TPU v7x, 32 devices: a whole 2x2x4 slice. The times are simulated.
32 devices in a mesh: cons: 4 (over y, x), blk: 8 (over z, core).
Axes of the slice: x: 2, y: 2, z: 4, core: 2. Of those that a mesh axis runs over, the one named last changes fastest.
Arguments:
- elevation: bfloat16 [16, 320, 6144], P('cons', 'blk'), may hold values from -6 to 6
- legendre: bfloat16 [320, 768, 768], P('blk', 'cons'), may hold values from -5 to 5, as said below
- cycle_weight: float32 [320], P('blk'), may hold values from 0.0003565902 to 0.0028527216
- love_factor: float32 [768], replicated, may hold values from 0.000390625 to 0.0052083335
- assignment: int32 [16], replicated, may hold values from 0 to 15, each once
Outputs:
- loading: float32 [16, 320, 6144], P('cons', 'blk')
Inputs may be any that keep to these rules, and one draw needn't show every extreme that they name: `legendre`: fully normalized associated Legendre functions (the square integrates to 1 over [-1, 1]) of each cycle's latitude, every cycle within 26 degrees of the equator; zero where the degree is below the order.
All inputs are finite; a program needn't handle non-finite values.
Results may differ from a plain program's by a relative error of at most 0.02.
Values may be sent and summed in bfloat16 or wider, within the bound.
A program may use at most 128 MiB of HBM per device.

v0:
```python
import functools

import jax
import jax.numpy as jnp
from jax import lax
from jax.experimental import pallas as pl
from jax.experimental.pallas import tpu as pltpu
from jax.sharding import PartitionSpec as P

GROUP = 16
LANES = 128
LEAD = 6
FIN = 4
REL0 = 8
REL1 = 14
RELN = 5
BACK = 4
SLACK = 2
AHEAD = 2
PACE = 3
CHUNKS = 3
MESH = pl.DeviceIdType.MESH


class Plan:
    def __init__(self, n_cons, n_blk, orders_dev, degrees):
        self.n_cons, self.chips = n_cons, n_blk // 2
        self.groups, self.columns = orders_dev // GROUP, degrees // LANES
        counts = [sum(self.width(c, g) for g in range(self.groups)) for c in range(n_cons)]
        self.counts = counts
        moved = [max(0, (counts[c] - counts[n_cons - 1 - c]) // 2) for c in range(n_cons)]
        self.moved = moved
        self.max_tiles = max(counts)
        self.max_moved = max(1, max(moved))
        self.queues = [counts[c] - moved[c] + moved[n_cons - 1 - c] for c in range(n_cons)]
        self.max_queue = max(self.queues)

    def first(self, c, g):
        return (c * self.groups + g) * GROUP // LANES

    def width(self, c, g):
        return self.columns - self.first(c, g)

    def starts(self, c):
        begin, out = 0, []
        for g in range(self.groups):
            out.append(begin)
            begin = begin + self.width(c, g)
        return out, begin

    def place(self, c, starts, t):
        g = 0
        for start in starts[1:]:
            g = g + jnp.where(t >= start, 1, 0)
        begin = 0
        for k in range(1, self.groups):
            begin = jnp.where(t >= starts[k], starts[k], begin)
        return g, (c * self.groups + g) * GROUP // LANES + t - begin


def pick(c, values):
    out = values[-1]
    for k in range(len(values) - 1):
        out = jnp.where(c == k, values[k], out)
    return out


def swap_blocks(tiles):
    count = LANES // GROUP
    block = lax.broadcasted_iota(jnp.int32, tiles[0].shape, len(tiles[0].shape) - 1) // GROUP
    step = count // 2
    while step:
        high = (block // step) % 2 == 1
        new = list(tiles)
        for a in range(count):
            if (a // step) % 2 == 0:
                low_t, high_t = tiles[a], tiles[a + step]
                up = pltpu.roll(high_t, GROUP * step, high_t.ndim - 1)
                down = pltpu.roll(low_t, LANES - GROUP * step, low_t.ndim - 1)
                new[a] = jnp.where(high, up, low_t)
                new[a + step] = jnp.where(high, high_t, down)
        tiles = new
        step //= 2
    return tiles


def sum_kernel(
    plan, x, love, order, legendre, out, table, table_sem, part, spread_s, whole, sent, taken, back, returned,
    pair_in, acc, given, inward_in, cross_in, coef, *sems
):
    (pair_s, pair_r, give_s, give_r, in_s, in_r, cross_s, cross_r, mid_s, out_s, coef_r, ret_s, ret_r, fin_s, fin_r) = sems[:15]
    there_s, there_r, home_s, home_r = sems[15:]
    me, c = lax.axis_index("blk"), lax.axis_index("cons")
    chips, half = plan.chips, part.shape[1] // 2
    n_cons, groups = plan.n_cons, plan.groups
    cycles = x.shape[1]
    blocks = LANES // GROUP
    folds = cycles // blocks
    rows = x.shape[2]
    all_rows = n_cons * rows
    pairs = plan.columns // 2
    p, core = me // 2, lax.rem(me, 2)
    mid = chips // 2
    left = p < mid
    depth = jnp.where(left, mid - 1 - p, p - mid)
    side = jnp.where(left, 0, 1)
    inner = jnp.where(left, me + 2, me - 2)
    outer = jnp.where(left, me - 2, me + 2)
    partner = me + 1 - 2 * core
    other_c = n_cons - 1 - c
    last = mid - 1

    starts, tiles = plan.starts(c)
    other_starts, _ = plan.starts(other_c)
    exports, imports = pick(c, plan.moved), pick(other_c, plan.moved)
    queue = pick(c, plan.queues)

    barrier = pltpu.get_barrier_semaphore()

    def greet(where):
        pl.semaphore_signal(barrier, inc=1, device_id=where, device_id_type=MESH)

    greet({"blk": partner})

    @pl.when(p > 0)
    def _():
        greet({"blk": me - 2})

    @pl.when(p < chips - 1)
    def _():
        greet({"blk": me + 2})

    peers = [lax.rem(c + k, n_cons) for k in range(1, n_cons)]
    for peer in peers:
        greet({"cons": peer})

    def loop(count, body):
        def step(i, carry):
            body(i)
            return carry

        lax.fori_loop(0, count, step, 0)

    def table_copy(g):
        return pltpu.make_async_copy(
            legendre.at[:, pl.ds(pl.multiple_of(g * GROUP, GROUP), GROUP), :], table.at[g], table_sem.at[g]
        )

    loop(groups, lambda g: table_copy(g).start())

    def pack(i):
        tile, fold = i // folds, lax.rem(i, folds)
        swapped = swap_blocks([x[tile, fold * blocks + k].astype(jnp.float32) for k in range(blocks)])
        for k in range(blocks):
            sent[tile * blocks + k, fold] = swapped[k].astype(sent.dtype)

    loop(x.shape[0] * folds, pack)

    heard = n_cons + jnp.where(p > 0, 1, 0) + jnp.where(p < chips - 1, 1, 0)
    pl.semaphore_wait(barrier, heard)

    def copy(src, dst, send, recv, where):
        return pltpu.make_async_remote_copy(
            src_ref=src, dst_ref=dst, send_sem=send, recv_sem=recv, device_id=where, device_id_type=MESH
        )

    chunk = groups // CHUNKS

    def there_copy(k, h, source):
        peer = peers[k]
        return copy(
            sent.at[pl.ds(peer * groups + h * chunk, chunk)],
            taken.at[source, pl.ds(h * chunk, chunk)],
            there_s.at[k, h],
            there_r.at[source, h],
            {"cons": peer},
        )

    for h in range(CHUNKS):
        for k in range(n_cons - 1):
            there_copy(k, h, c).start()

    def keep(g):
        taken[c, g] = sent[c * groups + g]

    loop(groups, keep)

    def home_copy(k, g, source):
        return copy(
            back.at[g, peers[k]],
            returned.at[source * groups + g],
            home_s.at[k, g],
            home_r.at[source * groups + g],
            {"cons": peers[k]},
        )

    def rows_of(k):
        return pl.ds(pl.multiple_of(k * half, half), half)

    mine, theirs = rows_of(core), rows_of(1 - core)

    def at(ref, spot, rows):
        g, lt = spot
        return ref.at[g, rows, pl.ds(pl.multiple_of(lt * LANES, LANES), LANES)]

    def pair_copy(t, spot):
        return copy(at(part, spot, theirs), pair_in.at[t], pair_s.at[t], pair_r.at[t], {"blk": partner})

    def give_copy(e):
        return copy(given.at[e], acc.at[LEAD + e], give_s.at[e], give_r.at[e], {"cons": other_c})

    def in_copy(q):
        return copy(acc.at[q], inward_in.at[q], in_s.at[q], in_r.at[q], {"blk": inner})

    def cross_copy(q):
        h = q // 2
        return copy(acc.at[q], cross_in.at[h], cross_s.at[h], cross_r.at[h], {"blk": inner})

    def mid_copy(q):
        return copy(coef.at[q], coef.at[q], mid_s.at[q // 2], coef_r.at[q], {"blk": inner})

    def out_copy(q):
        return copy(coef.at[q], coef.at[q], out_s.at[q], coef_r.at[q], {"blk": outer})

    def ret_copy(q, e, spot):
        return copy(coef.at[q], at(whole, spot, mine), ret_s.at[e], ret_r.at[e], {"cons": other_c})

    def fin_copy(t, spot):
        part_of = at(whole, spot, mine)
        return copy(part_of, part_of, fin_s.at[t], fin_r.at[t], {"blk": partner})

    def add(x, y):
        return x.astype(jnp.float32) + y.astype(jnp.float32)

    def is_import(q):
        return (q >= LEAD) & (q < LEAD + imports)

    def tile_of(q):
        return q + jnp.minimum(q + 1, exports) - jnp.where(q >= LEAD, imports, 0)

    def first_of(g):
        return (c * groups + g) * GROUP // LANES

    def start_of(g):
        out = tiles
        for k in range(groups - 1, -1, -1):
            out = jnp.where(g == k, starts[k], out)
        return out

    def lane_pair(lp):
        return pl.ds(pl.multiple_of(lp * 2 * LANES, 2 * LANES), 2 * LANES)

    def span(begin, end, body):
        def step(i, carry):
            body(i)
            return carry

        lax.fori_loop(begin, end, step, 0)

    lane = lax.broadcasted_iota(jnp.int32, (all_rows, LANES), 1) % GROUP

    def clear(g):
        first = first_of(g)

        def one(lt):
            whole[g, :, pl.ds(pl.multiple_of(lt * LANES, LANES), LANES)] = jnp.zeros((2 * half, LANES), whole.dtype)

        span(first // 2 * 2, first, one)

    loop(groups, clear)

    def produce(g):
        @pl.when(lax.rem(g, chunk) == 0)
        def _():
            for source in range(n_cons):

                @pl.when(c != source)
                def _():
                    there_copy(0, g // chunk, source).wait_recv()

        table_copy(g).wait()
        for fold in range(folds):
            parts = [taken[source, g, fold].astype(jnp.float32) for source in range(n_cons)]
            gathered = jnp.concatenate(parts, axis=0).astype(jnp.bfloat16)
            ordered = jnp.dot(order[...], gathered, preferred_element_type=jnp.float32)
            for m in range(GROUP):
                spread_s[pl.ds(m * all_rows, all_rows), pl.ds(fold * LANES, LANES)] = jnp.where(
                    lane == m, ordered, 0.0
                ).astype(spread_s.dtype)

        def one(lp):
            values = table[g, :, :, lane_pair(lp)].reshape(cycles * GROUP, 2 * LANES)
            part[g, :, lane_pair(lp)] = jnp.dot(
                spread_s[...], values, preferred_element_type=jnp.float32
            ).astype(part.dtype)

        span(first_of(g) // 2, pairs, one)
        span(start_of(g), start_of(g + 1), lambda t: pair_copy(t, plan.place(c, starts, t)).start())

    width = folds * LANES
    order_lane = lax.broadcasted_iota(jnp.int32, (rows, LANES), 1) % GROUP

    def restore(g):
        def take(t):
            fin_copy(t, plan.place(c, starts, t)).wait_recv()

        span(start_of(g), start_of(g + 1), take)

        def one(lp, total):
            values = table[g, :, :, lane_pair(lp)].reshape(cycles * GROUP, 2 * LANES)
            full = lax.dot_general(
                whole[g, :, lane_pair(lp)], values, (((1,), (1,)), ((), ())), preferred_element_type=jnp.float32
            )
            wide = lax.broadcasted_iota(jnp.int32, (all_rows, width), 1) % GROUP
            for m in range(GROUP):
                total = total + jnp.where(wide == m, full[m * all_rows : (m + 1) * all_rows], 0.0)
            return total

        total = lax.fori_loop(first_of(g) // 2, pairs, one, jnp.zeros((all_rows, width), jnp.float32))
        zero_order = (c * groups + g) * GROUP + order_lane == 0
        factor = jnp.where(zero_order, 1.0, 2.0)
        for peer in range(n_cons):
            for fold in range(folds):
                piece = total[peer * rows : (peer + 1) * rows, fold * LANES : (fold + 1) * LANES]
                back[g, peer, fold] = (piece * factor).astype(back.dtype)
        for k in range(n_cons - 1):
            home_copy(k, g, c).start()
        returned[c * groups + g] = back[g, c]

    def give(e):
        spot = plan.place(c, starts, 2 * e)
        pair_copy(2 * e, spot).wait_recv()
        given[e] = add(at(part, spot, mine)[...], pair_in[2 * e]).astype(given.dtype)
        give_copy(e).start()

    def gather(q):
        native = jnp.logical_not(is_import(q))

        @pl.when(native)
        def _():
            t = tile_of(q)
            spot = plan.place(c, starts, t)
            pair_copy(t, spot).wait_recv()
            acc[q] = add(at(part, spot, mine)[...], pair_in[t]).astype(acc.dtype)

        @pl.when(is_import(q))
        def _():
            give_copy(q - LEAD).wait_recv()

        @pl.when(depth < last)
        def _():
            in_copy(q).wait_recv()
            acc[q] = add(acc[q], inward_in[q]).astype(acc.dtype)

        @pl.when(depth > 0)
        def _():
            in_copy(q).start()

        @pl.when((depth == 0) & (lax.rem(q, 2) != side))
        def _():
            cross_copy(q).start()

    def spread(q):
        @pl.when(depth < last)
        def _():
            out_copy(q).start()

        @pl.when(is_import(q))
        def _():
            e = q - LEAD
            ret_copy(q, e, plan.place(other_c, other_starts, 2 * e)).start()

        @pl.when(jnp.logical_not(is_import(q)))
        def _():
            t = tile_of(q)
            spot = plan.place(c, starts, t)
            at(whole, spot, mine)[...] = coef[q]
            fin_copy(t, spot).start()

    def finish(q):
        @pl.when((depth == 0) & (lax.rem(q, 2) == side))
        def _():
            cross_copy(q).wait_recv()
            own = plan.place(c, starts, tile_of(q))[1]
            lent = plan.place(other_c, other_starts, 2 * (q - LEAD))[1]
            lt = jnp.where(is_import(q), lent, own)
            total = add(acc[q], cross_in[q // 2]) * love[pl.ds(lt, 1), :]
            coef[q] = total.astype(coef.dtype)
            mid_copy(q).start()
            spread(q)

    def relay(q):
        @pl.when((depth > 0) | (lax.rem(q, 2) != side))
        def _():
            out_copy(q).wait_recv()
            spread(q)

    def take_back(e):
        spot = plan.place(c, starts, 2 * e)
        ret_copy(0, e, spot).wait_recv()
        fin_copy(2 * e, spot).start()

    relay_gap = jnp.where(depth == 0, REL0, REL1 + (depth - 1) * RELN)
    back_gap = LEAD + relay_gap + BACK

    def ready(g):
        t = start_of(g + 1) - 1
        q = jnp.where(t >= LEAD, t + imports, t)
        q = jnp.where(exports > 0, t - exports, q)
        return jnp.where(t < 2 * exports, t // 2 + back_gap, q + relay_gap) + SLACK

    for g in range(AHEAD):
        produce(g)

    def step(i, done):
        ahead = AHEAD + i // PACE

        @pl.when((lax.rem(i, PACE) == 0) & (ahead < groups))
        def _():
            produce(ahead)

        @pl.when(i < exports)
        def _():
            give(i)

        @pl.when(i < queue)
        def _():
            gather(i)

        q = i - FIN

        @pl.when((q >= 0) & (q < queue))
        def _():
            finish(q)

        r = i - relay_gap

        @pl.when((r >= 0) & (r < queue))
        def _():
            relay(r)

        e = i - back_gap

        @pl.when((e >= 0) & (e < exports))
        def _():
            take_back(e)

        now = (done < groups) & (i >= ready(done))

        @pl.when(now)
        def _():
            restore(done)

        return done + jnp.where(now, 1, 0)

    count = plan.max_queue + LEAD + REL1 + mid * RELN + BACK
    done = lax.fori_loop(0, count, step, 0)
    span(done, groups, restore)

    def unpack(tile):
        def heard_from(k):
            index = tile * blocks + k

            @pl.when(index // groups != c)
            def _():
                home_copy(0, lax.rem(index, groups), index // groups).wait_recv()

        loop(blocks, heard_from)

        def one(fold):
            swapped = swap_blocks([returned[tile * blocks + k, fold].astype(jnp.float32) for k in range(blocks)])
            for k in range(blocks):
                out[tile, fold * blocks + k] = swapped[k].astype(out.dtype)

        loop(folds, one)

    loop(x.shape[0], unpack)

    def drain_tile(t):
        spot = plan.place(c, starts, t)
        pair_copy(t, spot).wait_send()
        fin_copy(t, spot).wait_send()

    loop(tiles, drain_tile)
    loop(exports, lambda e: give_copy(e).wait_send())

    def drain_queue(q):
        @pl.when(depth > 0)
        def _():
            in_copy(q).wait_send()

        @pl.when((depth == 0) & (lax.rem(q, 2) != side))
        def _():
            cross_copy(q).wait_send()

        @pl.when((depth == 0) & (lax.rem(q, 2) == side))
        def _():
            mid_copy(q).wait_send()

        @pl.when(depth < last)
        def _():
            out_copy(q).wait_send()

        @pl.when(is_import(q))
        def _():
            e = q - LEAD
            ret_copy(q, e, plan.place(other_c, other_starts, 2 * e)).wait_send()

    loop(queue, drain_queue)
    for k in range(n_cons - 1):
        for h in range(CHUNKS):
            there_copy(k, h, c).wait_send()

        loop(groups, lambda g, k=k: home_copy(k, g, c).wait_send())


def exchange(x, love, order, legendre, n_cons, n_blk):
    cycles, orders_dev, degrees = legendre.shape
    rows = x.shape[2]
    all_rows = n_cons * rows
    plan = Plan(n_cons, n_blk, orders_dev, degrees)
    groups, folds = plan.groups, cycles * GROUP // LANES
    half = (GROUP * all_rows // 2, LANES)
    kind = x.dtype
    tiles, queue, moved = plan.max_tiles, plan.max_queue, plan.max_moved
    halves = (queue + 1) // 2
    sems = [(n,) for n in [tiles] * 2 + [moved] * 2 + [queue] * 2 + [halves] * 2 + [halves, queue, queue] + [moved] * 2 + [tiles] * 2]
    sems += [(n_cons - 1, CHUNKS), (n_cons, CHUNKS), (n_cons - 1, groups), (n_cons * groups,)]
    lane_tiles = (folds, rows, LANES)
    vmem = pl.BlockSpec(memory_space=pltpu.VMEM)
    return pl.pallas_call(
        functools.partial(sum_kernel, plan),
        out_shape=jax.ShapeDtypeStruct(x.shape, kind),
        in_specs=[vmem] * 3 + [pl.BlockSpec(memory_space=pl.ANY)],
        out_specs=vmem,
        scratch_shapes=[
            pltpu.VMEM((groups, cycles, GROUP, degrees), kind),
            pltpu.SemaphoreType.DMA((groups,)),
            pltpu.VMEM((groups, GROUP * all_rows, degrees), kind),
            pltpu.VMEM((GROUP * all_rows, folds * LANES), kind),
            pltpu.VMEM((groups, GROUP * all_rows, degrees), kind),
            pltpu.VMEM((n_cons * groups,) + lane_tiles, kind),
            pltpu.VMEM((n_cons, groups) + lane_tiles, kind),
            pltpu.VMEM((groups, n_cons) + lane_tiles, kind),
            pltpu.VMEM((n_cons * groups,) + lane_tiles, kind),
            pltpu.VMEM((tiles,) + half, kind),
            pltpu.VMEM((queue,) + half, kind),
            pltpu.VMEM((moved,) + half, kind),
            pltpu.VMEM((queue,) + half, kind),
            pltpu.VMEM((halves,) + half, kind),
            pltpu.VMEM((queue,) + half, kind),
        ]
        + [pltpu.SemaphoreType.DMA(n) for n in sems],
        compiler_params=pltpu.CompilerParams(
            collective_id=0, has_side_effects=True, vmem_limit_bytes=60 * 2**20
        ),
    )(x, love.reshape(degrees // LANES, LANES), order, legendre)


def angles_of(lon_index, period, orders):
    order_index = jnp.arange(orders, dtype=jnp.int32)
    phases = lon_index[:, None] * order_index[None, :] % period
    angles = phases.astype(jnp.float32) * jnp.float32(2.0 * 3.141592653589793 / period)
    return jnp.cos(angles), jnp.sin(angles)


def quarter_table(length, period, orders):
    fine = 32
    coarse = length // fine
    parts = angles_of(jnp.arange(coarse, dtype=jnp.int32) * fine, period, orders)
    parts += angles_of(jnp.arange(fine, dtype=jnp.int32), period, orders)
    cos_a, sin_a, cos_b, sin_b = lax.optimization_barrier(parts)
    cos_a, sin_a = cos_a[:, None, :], sin_a[:, None, :]
    cosine = cos_a * cos_b[None] - sin_a * sin_b[None]
    minus_sine = -(sin_a * cos_b[None] + cos_a * sin_b[None])
    both = jnp.concatenate([cosine.astype(jnp.bfloat16), minus_sine.astype(jnp.bfloat16)], axis=2)
    return both.reshape(length, 2 * orders)


def local(elevation, legendre, cycle_weight, love_factor, assignment):
    fld_dev, cycle_dev, longitudes = elevation.shape
    orders_dev, degrees = legendre.shape[1:]
    orders = orders_dev * lax.axis_size("cons")
    quarter = longitudes // 4
    table = lax.optimization_barrier(quarter_table(quarter, longitudes, orders))
    residue = jnp.arange(orders, dtype=jnp.int32) % 4
    turn_re = (residue == 0).astype(jnp.float32) - (residue == 2).astype(jnp.float32)
    turn_im = (residue == 1).astype(jnp.float32) - (residue == 3).astype(jnp.float32)
    sign = turn_re * turn_re - turn_im * turn_im

    def halves(q):
        part = lax.slice_in_dim(elevation, q * quarter, (q + 1) * quarter, axis=2)
        both = jnp.einsum("fjk,kn->fjn", part, table, preferred_element_type=jnp.float32)
        return both[..., :orders], both[..., orders:]

    (re0, im0), (re1, im1), (re2, im2), (re3, im3) = (halves(q) for q in range(4))
    even_re, even_im = re0 + sign * re2, im0 + sign * im2
    odd_re, odd_im = re1 + sign * re3, im1 + sign * im3
    running = jnp.stack(
        [
            even_re + turn_re * odd_re + turn_im * odd_im,
            even_im + turn_re * odd_im - turn_im * odd_re,
        ],
        axis=1,
    )
    spectra = (running * cycle_weight[None, None, :, None]).astype(jnp.bfloat16)
    x = spectra.reshape(fld_dev, 2, cycle_dev, orders // LANES, LANES)
    x = x.transpose(3, 2, 1, 0, 4).reshape(orders // LANES, cycle_dev, 2 * fld_dev, LANES)
    n_cons = lax.axis_size("cons")
    row = jnp.arange(n_cons * 2 * fld_dev, dtype=jnp.int32)
    field, piece = row // (2 * fld_dev) * fld_dev + row % fld_dev, row // fld_dev % 2
    same = (assignment[field][:, None] == field[None, :]) & (piece[:, None] == piece[None, :])
    y = exchange(x, love_factor, same.astype(jnp.bfloat16), legendre, n_cons, lax.axis_size("blk"))
    y = y.reshape(orders // LANES, cycle_dev, 2, fld_dev, LANES).transpose(2, 3, 1, 0, 4)
    y = y.reshape(2, fld_dev, cycle_dev, orders).astype(jnp.float32)
    re, im = y[0], y[1]
    turned = [
        (re, im),
        (turn_re * re - turn_im * im, turn_re * im + turn_im * re),
        (sign * re, sign * im),
        (turn_re * re + turn_im * im, turn_re * im - turn_im * re),
    ]
    return jnp.concatenate(
        [
            jnp.einsum(
                "fjn,kn->fjk",
                jnp.concatenate(pair, axis=2).astype(jnp.bfloat16),
                table,
                preferred_element_type=jnp.float32,
            )
            for pair in turned
        ],
        axis=2,
    )


def solution(mesh):
    placed = (P("cons", "blk", None), P("blk", "cons", None), P("blk"), P(), P())
    return jax.shard_map(
        local, mesh=mesh, in_specs=placed, out_specs=P("cons", "blk", None), check_vma=False
    )
```

profile of v0, /device:TPU:1, one launch (start us, length us, event | category | flops | bytes accessed | tf_op | source)
XLA Modules:
  0.0 141.8 jit_solution(10928719129851672718)
XLA Ops:
  0.0 0.0 copy-start
  0.0 0.7 fusion.58
  0.7 0.4 fusion.65
  1.1 2.2 %subtract_convert_fusion = (bf16[48,32,768]{2,1,0:T(8,128)(2,1)S(1)}, bf16[48,32,768]{2,1,0:T(8,128)(2,1)S(1)}) fusion(f32[32,768]{1,0:T(8,128)S(1)} %get-tuple-element.12, f32[48,768]{1,0:T(8,128)S(1)} %get-tuple-element.11, f32[32,768]{1,0:T(8,128)S(1)} %get-tuple-element.10, f32[48,768]{1,0:T(8,128)S(1)} %get-tuple-element.9), kind=kLoop, calls=%fused_computation.19 | loop fusion | flops 10616832 | bytes 5210112 | tf_op jit(solution)/shard_map/convert_element_type | solution.py:576
  3.3 0.0 copy-start.3
  3.3 0.4 pad_maximum_fusion
  3.7 1.2 copy-done.3
  4.8 0.0 copy-start.1
  4.8 0.9 fusion.16
  5.8 0.9 fusion.19
  6.7 0.9 fusion.22
  7.6 0.0 copy-done.1
  7.6 0.9 fusion.25
  8.6 0.0 copy-start.2
  8.6 0.3 fusion.37
  8.9 0.1 stack.10
  9.0 0.1 stack.9
  9.0 0.2 copy-done.2
  9.2 0.2 fusion.29
  9.4 1.2 copy.10
  10.6 0.0 copy-done
  10.6 0.7 gather_fusion
  11.3 0.7 and_convert_fusion.order
  12.0 116.4 %shard_map.55 = bf16[6,40,8,128]{3,2,1,0:T(8,128)(2,1)} custom-call(bf16[6,40,8,128]{3,2,1,0:T(8,128)(2,1)} %bitcast.53, f32[6,128]{1,0:T(8,128)} %bitcast.55, bf16[32,32]{1,0:T(8,128)(2,1)} %and_convert_fusion.order, bf16[40,192,768]{2,1,0:T(8,128)(2,1)} %legendre.1), custom_call_target="tpu_custom_call" | custom-call | tf_op jit(solution)/shard_map/pallas_call | solution.py:531
  128.4 1.3 copy.13
  129.8 0.0 slice-start
  129.8 0.1 fusion.85
  129.9 0.1 squeeze.6
  130.0 0.1 squeeze.7
  130.1 0.0 slice-start.1
  130.1 0.3 fusion.86
  130.5 4.2 %fusion.6 = f32[4,40,1536]{2,1,0:T(8,128)S(1)} fusion(bf16[1536,1536]{1,0:T(8,128)(2,1)} %copy-done.1, bf16[4,40,768]{2,1,0:T(8,128)(2,1)S(1)} %get-tuple-element.28, bf16[4,40,768]{2,1,0:T(8,128)(2,1)S(1)} %get-tuple-element.21), kind=kOutput, calls=%fused_computation.8 | convolution fusion | flops 755957760 | bytes 6193152 | tf_op jit(solution)/shard_map/fjn,kn->fjk/dot_general | solution.py:625
  134.6 0.0 slice-done
  134.6 0.0 slice-done.1
  134.6 1.7 %fusion.4 = f32[4,40,1536]{2,1,0:T(8,128)S(1)} fusion(bf16[1536,1536]{1,0:T(8,128)(2,1)S(1)} %bitcast.49, bf16[4,40,768]{2,1,0:T(8,128)(2,1)S(1)} %get-tuple-element.23, bf16[4,40,768]{2,1,0:T(8,128)(2,1)S(1)} %get-tuple-element.26), kind=kOutput, calls=%fused_computation.6 | convolution fusion | flops 755957760 | bytes 6193152 | tf_op jit(solution)/shard_map/fjn,kn->fjk/dot_general | solution.py:625
  136.3 1.7 %fusion.2 = f32[4,40,1536]{2,1,0:T(8,128)S(1)} fusion(bf16[1536,1536]{1,0:T(8,128)(2,1)S(1)} %bitcast.49, bf16[4,40,768]{2,1,0:T(8,128)(2,1)S(1)} %get-tuple-element.27, bf16[4,40,768]{2,1,0:T(8,128)(2,1)S(1)} %get-tuple-element.22), kind=kOutput, calls=%fused_computation.4 | convolution fusion | flops 755957760 | bytes 6193152 | tf_op jit(solution)/shard_map/fjn,kn->fjk/dot_general | solution.py:625
  138.0 1.7 %fusion = f32[4,40,1536]{2,1,0:T(8,128)S(1)} fusion(bf16[1536,1536]{1,0:T(8,128)(2,1)S(1)} %bitcast.49, bf16[4,40,768]{2,1,0:T(8,128)(2,1)S(1)} %get-tuple-element.24, bf16[4,40,768]{2,1,0:T(8,128)(2,1)S(1)} %get-tuple-element.25), kind=kOutput, calls=%fused_computation.2 | convolution fusion | flops 755957760 | bytes 6193152 | tf_op jit(solution)/shard_map/fjn,kn->fjk/dot_general | solution.py:625
  139.6 2.2 %pad_maximum_fusion.1 = f32[4,40,6144]{2,1,0:T(8,128)} fusion(f32[4,40,1536]{2,1,0:T(8,128)S(1)} %fusion, f32[4,40,1536]{2,1,0:T(8,128)S(1)} %fusion.2, f32[4,40,1536]{2,1,0:T(8,128)S(1)} %fusion.4, f32[4,40,1536]{2,1,0:T(8,128)S(1)} %fusion.6), kind=kLoop, calls=%fused_computation.20 | loop fusion | flops 2949120 | bytes 7864320 | tf_op jit(solution)/shard_map/concatenate | solution.py:623
  (7 shorter events, 0.0 us)
Async XLA Ops:
  0.0 10.6 %copy-start = (s32[16]{0:T(128)S(1)}, s32[16]{0:T(128)}, u32[]{:S(2)}) copy-start(s32[16]{0:T(128)} %param.9) | copy-start | bytes 196
  3.3 1.5 %copy-start.3 = (bf16[4,40,6144]{2,1,0:T(8,128)(2,1)S(1)}, bf16[4,40,6144]{2,1,0:T(8,128)(2,1)}, u32[]{:S(2)}) copy-start(bf16[4,40,6144]{2,1,0:T(8,128)(2,1)} %param.5) | copy-start | bytes 5898244
  4.8 2.8 %copy-start.1 = (bf16[1536,1536]{1,0:T(8,128)(2,1)}, bf16[1536,1536]{1,0:T(8,128)(2,1)S(1)}, u32[]{:S(2)}) copy-start(bf16[1536,1536]{1,0:T(8,128)(2,1)S(1)} %pad_maximum_fusion) | copy-start | bytes 14155780
  8.6 0.7 copy-start.2
  129.8 4.9 %slice-start = ((s8[4718592]{0:T(1024)(128)(4,1)}), s8[524288]{0:T(1024)(128)(4,1)S(1)}, s32[]{:S(2)}) async-start(s8[4718592]{0:T(1024)(128)(4,1)} %bitcast.48), calls=%async_computation | async-start | bytes 1048576
  130.1 4.5 %slice-start.1 = ((s8[4718592]{0:T(1024)(128)(4,1)}), s8[4194304]{0:T(1024)(128)(4,1)S(1)}, s32[]{:S(2)}) async-start(s8[4718592]{0:T(1024)(128)(4,1)} %bitcast.48), calls=%async_computation.1 | async-start | bytes 8388608
where the time goes:
time: 142 us
  Pallas kernels  116 us (82%)
  matrix products  12.8 us (9%)
  other arithmetic  7.35 us (5%)
  local copies, waits for them, and re-layouts  5.02 us (4%)
    pallas_call x1, Pallas kernels, exchange(): pl.pallas_call(functools.partial(sum_kernel, plan), out_shape=jax.ShapeDt...  116 us
    dot_general x4, matrix products, local(): jnp.einsum('fjn,kn->fjk', jnp.concatenate(pair, axis=2).astype(jnp.bfloat...  9.12 us
    dot_general x4, matrix products, halves(): jnp.einsum('fjk,kn->fjn', part, table, preferred_element_type=jnp.float32)  3.68 us

commit v1 on v0

--- a/solution.py
+++ b/solution.py
@@ -19,6 +19,8 @@
 AHEAD = 2
 PACE = 3
 CHUNKS = 3
+WAVE_AT = 1
+FINE = 32
 MESH = pl.DeviceIdType.MESH
 
 
@@ -85,8 +87,8 @@
 
 
 def sum_kernel(
-    plan, x, love, order, legendre, out, table, table_sem, part, spread_s, whole, sent, taken, back, returned,
-    pair_in, acc, given, inward_in, cross_in, coef, *sems
+    plan, x, love, order, legendre, out, wave, table, table_sem, part, spread_s, whole, sent, taken, back, returned,
+    pair_in, acc, given, inward_in, cross_in, coef, fine, waves, wave_sem, *sems
 ):
     (pair_s, pair_r, give_s, give_r, in_s, in_r, cross_s, cross_r, mid_s, out_s, coef_r, ret_s, ret_r, fin_s, fin_r) = sems[:15]
     there_s, there_r, home_s, home_r = sems[15:]
@@ -148,13 +150,13 @@
 
     loop(groups, lambda g: table_copy(g).start())
 
-    def pack(i):
-        tile, fold = i // folds, lax.rem(i, folds)
-        swapped = swap_blocks([x[tile, fold * blocks + k].astype(jnp.float32) for k in range(blocks)])
+    def pack(tile):
+        split = x[tile].astype(jnp.float32).reshape(folds, blocks, rows, LANES)
+        swapped = swap_blocks([split[:, k] for k in range(blocks)])
         for k in range(blocks):
-            sent[tile * blocks + k, fold] = swapped[k].astype(sent.dtype)
-
-    loop(x.shape[0] * folds, pack)
+            sent[tile * blocks + k] = swapped[k].astype(sent.dtype)
+
+    loop(x.shape[0], pack)
 
     heard = n_cons + jnp.where(p > 0, 1, 0) + jnp.where(p < chips - 1, 1, 0)
     pl.semaphore_wait(barrier, heard)
@@ -194,6 +196,8 @@
             {"cons": peers[k]},
         )
 
+    corner = (0, plan.columns - 1)
+
     def rows_of(k):
         return pl.ds(pl.multiple_of(k * half, half), half)
 
@@ -302,7 +306,7 @@
 
     def restore(g):
         def take(t):
-            fin_copy(t, plan.place(c, starts, t)).wait_recv()
+            fin_copy(t, corner).wait_recv()
 
         span(start_of(g), start_of(g + 1), take)
 
@@ -409,10 +413,47 @@
         q = jnp.where(exports > 0, t - exports, q)
         return jnp.where(t < 2 * exports, t // 2 + back_gap, q + relay_gap) + SLACK
 
+    quarter = waves.shape[2]
+    fine_rows = fine.shape[1]
+    wave_blocks = waves.shape[1] // fine_rows
+
+    def wave_copy(b):
+        rows_here = pl.ds(pl.multiple_of(b * fine_rows, fine_rows), fine_rows)
+        return pltpu.make_async_copy(waves.at[:, rows_here, :], wave.at[:, rows_here, :], wave_sem.at[b])
+
+    def turn(row):
+        lon = lax.broadcasted_iota(jnp.int32, row.shape, 1).astype(jnp.float32)
+        phase = row.astype(jnp.float32) * lon
+        period = 4.0 * quarter
+        phase = phase - jnp.floor(phase * (1.0 / period)) * period
+        angle = phase * (2.0 * 3.141592653589793 / period)
+        return jnp.cos(angle), jnp.sin(angle)
+
+    def make_fine():
+        fine[0], fine[1] = turn(lax.broadcasted_iota(jnp.int32, (fine_rows, quarter), 0))
+
+    def make_wave(b):
+        cos_a, sin_a = turn(jnp.full((8, quarter), b * fine_rows, jnp.int32))
+        cos_a, sin_a = cos_a[:1], sin_a[:1]
+        here = pl.ds(pl.multiple_of(b * fine_rows, fine_rows), fine_rows)
+        waves[0, here, :] = (cos_a * fine[0] - sin_a * fine[1]).astype(waves.dtype)
+        waves[1, here, :] = (-sin_a * fine[0] - cos_a * fine[1]).astype(waves.dtype)
+        wave_copy(b).start()
+
     for g in range(AHEAD):
         produce(g)
 
     def step(i, done):
+        @pl.when(i == WAVE_AT)
+        def _():
+            make_fine()
+
+        b = i - WAVE_AT - 1
+
+        @pl.when((b >= 0) & (b < wave_blocks))
+        def _():
+            make_wave(b)
+
         ahead = AHEAD + i // PACE
 
         @pl.when((lax.rem(i, PACE) == 0) & (ahead < groups))
@@ -467,19 +508,15 @@
 
         loop(blocks, heard_from)
 
-        def one(fold):
-            swapped = swap_blocks([returned[tile * blocks + k, fold].astype(jnp.float32) for k in range(blocks)])
-            for k in range(blocks):
-                out[tile, fold * blocks + k] = swapped[k].astype(out.dtype)
-
-        loop(folds, one)
+        swapped = swap_blocks([returned[tile * blocks + k].astype(jnp.float32) for k in range(blocks)])
+        merged = jnp.stack(swapped, axis=1).reshape(cycles * rows, LANES)
+        out[pl.ds(pl.multiple_of(tile * cycles * rows, 8), cycles * rows), :] = merged
 
     loop(x.shape[0], unpack)
 
     def drain_tile(t):
-        spot = plan.place(c, starts, t)
-        pair_copy(t, spot).wait_send()
-        fin_copy(t, spot).wait_send()
+        pair_copy(t, corner).wait_send()
+        fin_copy(t, corner).wait_send()
 
     loop(tiles, drain_tile)
     loop(exports, lambda e: give_copy(e).wait_send())
@@ -504,9 +541,10 @@
         @pl.when(is_import(q))
         def _():
             e = q - LEAD
-            ret_copy(q, e, plan.place(other_c, other_starts, 2 * e)).wait_send()
+            ret_copy(q, e, corner).wait_send()
 
     loop(queue, drain_queue)
+    loop(wave_blocks, lambda b: wave_copy(b).wait())
     for k in range(n_cons - 1):
         for h in range(CHUNKS):
             there_copy(k, h, c).wait_send()
@@ -514,7 +552,7 @@
         loop(groups, lambda g, k=k: home_copy(k, g, c).wait_send())
 
 
-def exchange(x, love, order, legendre, n_cons, n_blk):
+def exchange(x, love, order, legendre, quarter, n_cons, n_blk):
     cycles, orders_dev, degrees = legendre.shape
     rows = x.shape[2]
     all_rows = n_cons * rows
@@ -527,12 +565,16 @@
     sems = [(n,) for n in [tiles] * 2 + [moved] * 2 + [queue] * 2 + [halves] * 2 + [halves, queue, queue] + [moved] * 2 + [tiles] * 2]
     sems += [(n_cons - 1, CHUNKS), (n_cons, CHUNKS), (n_cons - 1, groups), (n_cons * groups,)]
     lane_tiles = (folds, rows, LANES)
+    waves = (2, x.shape[0] * LANES, quarter)
     vmem = pl.BlockSpec(memory_space=pltpu.VMEM)
     return pl.pallas_call(
         functools.partial(sum_kernel, plan),
-        out_shape=jax.ShapeDtypeStruct(x.shape, kind),
+        out_shape=[
+            jax.ShapeDtypeStruct((x.shape[0] * x.shape[1] * rows, LANES), jnp.float32),
+            jax.ShapeDtypeStruct(waves, kind),
+        ],
         in_specs=[vmem] * 3 + [pl.BlockSpec(memory_space=pl.ANY)],
-        out_specs=vmem,
+        out_specs=[vmem, pl.BlockSpec(memory_space=pl.ANY)],
         scratch_shapes=[
             pltpu.VMEM((groups, cycles, GROUP, degrees), kind),
             pltpu.SemaphoreType.DMA((groups,)),
@@ -549,12 +591,95 @@
             pltpu.VMEM((queue,) + half, kind),
             pltpu.VMEM((halves,) + half, kind),
             pltpu.VMEM((queue,) + half, kind),
+            pltpu.VMEM((2, FINE, quarter), jnp.float32),
+            pltpu.VMEM(waves, kind),
+            pltpu.SemaphoreType.DMA((waves[1] // FINE,)),
         ]
         + [pltpu.SemaphoreType.DMA(n) for n in sems],
         compiler_params=pltpu.CompilerParams(
             collective_id=0, has_side_effects=True, vmem_limit_bytes=60 * 2**20
         ),
     )(x, love.reshape(degrees // LANES, LANES), order, legendre)
+
+
+def inverse_kernel(y, wave, loading, lhs, held, result, wave_sem, out_sem):
+    fields, cycles, longitudes = loading.shape
+    quarter, tiles = longitudes // 4, lhs.shape[1] // LANES
+    width, parts = held.shape[3], held.shape[0]
+    rows = 2 * fields
+
+    def columns(n):
+        return pl.ds(pl.multiple_of(n * width, width), width)
+
+    def wave_copy(n):
+        return pltpu.make_async_copy(wave.at[:, :, columns(n)], held.at[n], wave_sem.at[n])
+
+    def out_copy(n, q):
+        place = pl.ds(pl.multiple_of(q * quarter + n * width, width), width)
+        return pltpu.make_async_copy(
+            result.at[n, pl.ds(q * fields, fields)], loading.at[:, :, place], out_sem.at[n, q]
+        )
+
+    for n in range(parts):
+        wave_copy(n).start()
+    residue = lax.broadcasted_iota(jnp.int32, (2 * cycles, LANES), 1) % 4
+    turn_re = jnp.where(residue == 0, 1.0, jnp.where(residue == 2, -1.0, 0.0))
+    turn_im = jnp.where(residue == 1, 1.0, jnp.where(residue == 3, -1.0, 0.0))
+    sign = turn_re * turn_re - turn_im * turn_im
+    orders = tiles * LANES // 2
+    for tile in range(tiles // 2):
+
+        def load(piece, pair):
+            at = [tile * cycles * rows + piece * fields + 2 * pair + k for k in range(2)]
+            return jnp.concatenate([y[pl.ds(a, cycles, stride=rows), :] for a in at], axis=0)
+
+        for pair in range(fields // 2):
+            re, im = load(0, pair), load(1, pair)
+            turned = (
+                (re, im),
+                (turn_re * re - turn_im * im, turn_re * im + turn_im * re),
+                (sign * re, sign * im),
+                (turn_re * re + turn_im * im, turn_re * im - turn_im * re),
+            )
+            for q in range(4):
+                here = pl.ds((q * (fields // 2) + pair) * 2 * cycles, 2 * cycles)
+                for piece in range(2):
+                    lanes = pl.ds(piece * orders + tile * LANES, LANES)
+                    lhs[here, lanes] = turned[q][piece].astype(lhs.dtype)
+
+    def one(n, carry):
+        wave_copy(n).wait()
+        table = held[n].reshape(2 * orders, width)
+        product = jnp.dot(lhs[...], table, preferred_element_type=jnp.float32)
+        result[n] = product.reshape(4 * fields, cycles, width)
+        for q in range(4):
+            out_copy(n, q).start()
+        return carry
+
+    lax.fori_loop(0, parts, one, 0)
+    for n in range(parts):
+        for q in range(4):
+            out_copy(n, q).wait()
+
+
+def inverse(y, wave, fields, cycles):
+    orders, quarter = wave.shape[1:]
+    parts = quarter // (2 * LANES)
+    anywhere = pl.BlockSpec(memory_space=pl.ANY)
+    return pl.pallas_call(
+        inverse_kernel,
+        out_shape=jax.ShapeDtypeStruct((fields, cycles, 4 * quarter), jnp.float32),
+        in_specs=[pl.BlockSpec(memory_space=pltpu.VMEM), anywhere],
+        out_specs=anywhere,
+        scratch_shapes=[
+            pltpu.VMEM((4 * fields * cycles, 2 * orders), jnp.bfloat16),
+            pltpu.VMEM((parts, 2, orders, 2 * LANES), jnp.bfloat16),
+            pltpu.VMEM((parts, 4 * fields, cycles, 2 * LANES), jnp.float32),
+            pltpu.SemaphoreType.DMA((parts,)),
+            pltpu.SemaphoreType.DMA((parts, 4)),
+        ],
+        compiler_params=pltpu.CompilerParams(vmem_limit_bytes=40 * 2**20),
+    )(y, wave)
 
 
 def angles_of(lon_index, period, orders):
@@ -607,31 +732,14 @@
     x = spectra.reshape(fld_dev, 2, cycle_dev, orders // LANES, LANES)
     x = x.transpose(3, 2, 1, 0, 4).reshape(orders // LANES, cycle_dev, 2 * fld_dev, LANES)
     n_cons = lax.axis_size("cons")
-    row = jnp.arange(n_cons * 2 * fld_dev, dtype=jnp.int32)
-    field, piece = row // (2 * fld_dev) * fld_dev + row % fld_dev, row // fld_dev % 2
-    same = (assignment[field][:, None] == field[None, :]) & (piece[:, None] == piece[None, :])
-    y = exchange(x, love_factor, same.astype(jnp.bfloat16), legendre, n_cons, lax.axis_size("blk"))
-    y = y.reshape(orders // LANES, cycle_dev, 2, fld_dev, LANES).transpose(2, 3, 1, 0, 4)
-    y = y.reshape(2, fld_dev, cycle_dev, orders).astype(jnp.float32)
-    re, im = y[0], y[1]
-    turned = [
-        (re, im),
-        (turn_re * re - turn_im * im, turn_re * im + turn_im * re),
-        (sign * re, sign * im),
-        (turn_re * re + turn_im * im, turn_re * im - turn_im * re),
-    ]
-    return jnp.concatenate(
-        [
-            jnp.einsum(
-                "fjn,kn->fjk",
-                jnp.concatenate(pair, axis=2).astype(jnp.bfloat16),
-                table,
-                preferred_element_type=jnp.float32,
-            )
-            for pair in turned
-        ],
-        axis=2,
-    )
+    slots = (n_cons, 2, fld_dev)
+    field = jnp.arange(n_cons * fld_dev, dtype=jnp.int32).reshape(n_cons, 1, fld_dev)
+    chosen = assignment.reshape(n_cons, 1, fld_dev)
+    piece = jnp.arange(2, dtype=jnp.int32).reshape(1, 2, 1)
+    give, have = jnp.broadcast_to(2 * field + piece, slots), jnp.broadcast_to(2 * chosen + piece, slots)
+    order = (have.reshape(-1, 1) == give.reshape(1, -1)).astype(jnp.bfloat16)
+    y, wave = exchange(x, love_factor, order, legendre, quarter, n_cons, lax.axis_size("blk"))
+    return inverse(y, wave, fld_dev, cycle_dev)
 
 
 def solution(mesh):

time: 142 us -> 129 us (0.908)
  matrix products: 12.8 us -> 3.68 us
  Pallas kernels: 116 us -> 113 us
  other arithmetic: 7.35 us -> 5.39 us
  local copies, waits for them, and re-layouts: 5.02 us -> 6.48 us
    dot_general x4 -> x0, matrix products: 9.12 us -> none  [local(): jnp.einsum('fjn,kn->fjk', jnp.concatenate(pair, axis=2).astype(jnp.bfloat...]
    unnamed x12 -> x8, local copies, waits for them, and re-layouts: 1.37 us -> 4.91 us
    pallas_call x1 -> x2, Pallas kernels: 116 us -> 113 us  [the longest x1 107 us: exchange(): pl.pallas_call(functools.partial(sum_kernel, plan), out_shape=[jax.ShapeD...]
    concatenate x1 -> x0, other arithmetic: 2.2 us -> none  [local(): jnp.concatenate([jnp.einsum('fjn,kn->fjk', jnp.concatenate(pair, axis=2)....]
where the time goes in v1:
time: 129 us
  Pallas kernels  113 us (88%)
  local copies, waits for them, and re-layouts  6.48 us (5%)
  other arithmetic  5.39 us (4%)
  matrix products  3.68 us (3%)
    pallas_call x1, Pallas kernels, exchange(): pl.pallas_call(functools.partial(sum_kernel, plan), out_shape=[jax.ShapeD...  107 us
    pallas_call x1, Pallas kernels, inverse(): pl.pallas_call(inverse_kernel, out_shape=jax.ShapeDtypeStruct((fields, cy...  5.91 us
    unnamed x8, local copies, waits for them, and re-layouts  4.91 us
    dot_general x4, matrix products, halves(): jnp.einsum('fjk,kn->fjn', part, table, preferred_element_type=jnp.float32)  3.68 us

profile of v1, /device:TPU:1, one launch (start us, length us, event | category | flops | bytes accessed | tf_op | source)
XLA Modules:
  0.0 128.8 jit_solution(13798653408193800039)
XLA Ops:
  0.0 0.7 broadcast_multiply_fusion
  0.7 0.1 mul.272
  0.8 0.1 add.135
  0.9 0.1 add.139
  1.0 0.7 compare_convert_fusion.order
  1.6 0.4 fusion.45
  2.0 0.7 fusion.38
  2.7 2.1 %subtract_convert_fusion = (bf16[48,32,768]{2,1,0:T(8,128)(2,1)S(1)}, bf16[48,32,768]{2,1,0:T(8,128)(2,1)S(1)}) fusion(f32[32,768]{1,0:T(8,128)S(1)} %get-tuple-element.14, f32[48,768]{1,0:T(8,128)S(1)} %get-tuple-element.13, f32[32,768]{1,0:T(8,128)S(1)} %get-tuple-element.12, f32[48,768]{1,0:T(8,128)S(1)} %get-tuple-element.11), kind=kLoop, calls=%fused_computation.10 | loop fusion | flops 10616832 | bytes 5210112 | tf_op jit(solution)/shard_map/convert_element_type | solution.py:701
  4.8 0.0 copy-start.3
  4.9 0.4 pad_maximum_fusion
  5.2 1.2 copy-done.3
  6.4 0.9 fusion.11
  7.3 0.9 fusion.14
  8.2 0.9 fusion.17
  9.2 0.9 fusion.8
  10.1 0.0 copy-start.2
  10.1 0.3 fusion.29
  10.4 0.1 stack.9
  10.5 0.1 stack.10
  10.6 0.2 copy-done.2
  10.8 0.2 fusion.21
  11.0 1.2 copy.8
  12.1 107.0 %shard_map.55 = (f32[1920,128]{1,0:T(8,128)}, bf16[2,768,1536]{2,1,0:T(8,128)(2,1)}) custom-call(bf16[6,40,8,128]{3,2,1,0:T(8,128)(2,1)} %bitcast.33, f32[6,128]{1,0:T(8,128)} %bitcast.34, bf16[32,32]{1,0:T(8,128)(2,1)} %compare_convert_fusion.order, bf16[40,192,768]{2,1,0:T(8,128)(2,1)} %legendre.1), custom_call_target="tpu_custom_call" | custom-call | tf_op jit(solution)/shard_map/pallas_call | solution.py:570
  119.2 0.0 copy-start
  119.2 2.3 %copy-done = bf16[2,768,1536]{2,1,0:T(8,128)(2,1)S(1)} copy-done((bf16[2,768,1536]{2,1,0:T(8,128)(2,1)S(1)}, bf16[2,768,1536]{2,1,0:T(8,128)(2,1)}, u32[]{:S(2)}) %copy-start) | copy-done | bytes 4718616
  121.5 0.0 copy-start.1
  121.5 1.2 copy-done.1
  122.7 5.9 %shard_map.56 = f32[4,40,6144]{2,1,0:T(8,128)} custom-call(f32[1920,128]{1,0:T(8,128)S(1)} %copy-done.1, bf16[2,768,1536]{2,1,0:T(8,128)(2,1)S(1)} %copy-done), custom_call_target="tpu_custom_call" | custom-call | tf_op jit(solution)/shard_map/pallas_call | solution.py:669
  (6 shorter events, 0.0 us)
Async XLA Ops:
  4.8 1.5 %copy-start.3 = (bf16[4,40,6144]{2,1,0:T(8,128)(2,1)S(1)}, bf16[4,40,6144]{2,1,0:T(8,128)(2,1)}, u32[]{:S(2)}) copy-start(bf16[4,40,6144]{2,1,0:T(8,128)(2,1)} %param.5) | copy-start | bytes 5898244
  10.1 0.7 copy-start.2
  119.2 2.3 %copy-start = (bf16[2,768,1536]{2,1,0:T(8,128)(2,1)S(1)}, bf16[2,768,1536]{2,1,0:T(8,128)(2,1)}, u32[]{:S(2)}) copy-start(bf16[2,768,1536]{2,1,0:T(8,128)(2,1)} %get-tuple-element.16.wave) | copy-start | bytes 14155780
  121.5 1.2 copy-start.1

commit v2 on v1

--- a/solution.py
+++ b/solution.py
@@ -87,18 +87,21 @@
 
 
 def sum_kernel(
-    plan, x, love, order, legendre, out, wave, table, table_sem, part, spread_s, whole, sent, taken, back, returned,
-    pair_in, acc, given, inward_in, cross_in, coef, fine, waves, wave_sem, *sems
+    plan, elevation, weight, assignment, love, legendre, out, wave, table, table_sem, part, spread_s, whole, sent, taken, back, returned,
+    pair_in, acc, given, inward_in, cross_in, coef, fine, waves, wave_sem,
+    field_sem, coarse, near, forward, weights, order, split_s, *sems
 ):
     (pair_s, pair_r, give_s, give_r, in_s, in_r, cross_s, cross_r, mid_s, out_s, coef_r, ret_s, ret_r, fin_s, fin_r) = sems[:15]
     there_s, there_r, home_s, home_r = sems[15:]
     me, c = lax.axis_index("blk"), lax.axis_index("cons")
     chips, half = plan.chips, part.shape[1] // 2
     n_cons, groups = plan.n_cons, plan.groups
-    cycles = x.shape[1]
+    cycles = weight.shape[0]
     blocks = LANES // GROUP
     folds = cycles // blocks
-    rows = x.shape[2]
+    fields = elevation.shape[0] // cycles
+    rows = 2 * fields
+    order_tiles = n_cons * groups // blocks
     all_rows = n_cons * rows
     pairs = plan.columns // 2
     p, core = me // 2, lax.rem(me, 2)
@@ -148,19 +151,6 @@
             legendre.at[:, pl.ds(pl.multiple_of(g * GROUP, GROUP), GROUP), :], table.at[g], table_sem.at[g]
         )
 
-    loop(groups, lambda g: table_copy(g).start())
-
-    def pack(tile):
-        split = x[tile].astype(jnp.float32).reshape(folds, blocks, rows, LANES)
-        swapped = swap_blocks([split[:, k] for k in range(blocks)])
-        for k in range(blocks):
-            sent[tile * blocks + k] = swapped[k].astype(sent.dtype)
-
-    loop(x.shape[0], pack)
-
-    heard = n_cons + jnp.where(p > 0, 1, 0) + jnp.where(p < chips - 1, 1, 0)
-    pl.semaphore_wait(barrier, heard)
-
     def copy(src, dst, send, recv, where):
         return pltpu.make_async_remote_copy(
             src_ref=src, dst_ref=dst, send_sem=send, recv_sem=recv, device_id=where, device_id_type=MESH
@@ -178,7 +168,99 @@
             {"cons": peer},
         )
 
+    quarter = waves.shape[2]
+    period = 4.0 * quarter
+    slot_lanes = whole.shape[2]
+    per_quarter = quarter // slot_lanes
+    chunk_orders = chunk * GROUP
+    half_lanes = n_cons * chunk_orders
+    lens = coarse.shape[1]
+
+    def circle(phase):
+        phase = phase - jnp.floor(phase * (1.0 / period)) * period
+        angle = phase * (2.0 * 3.141592653589793 / period)
+        return jnp.cos(angle), jnp.sin(angle)
+
+    def field_copy(i):
+        lanes = pl.ds(i * slot_lanes, slot_lanes)
+        return pltpu.make_async_copy(
+            elevation.at[:, lanes], whole.at[i, pl.ds(0, elevation.shape[0]), :], field_sem.at[i]
+        )
+
+    for i in range(4 * per_quarter):
+        field_copy(i).start()
+    loop(groups, lambda g: table_copy(g).start())
+
+    def set_weight(j):
+        weights[pl.ds(j, 1), :] = jnp.full((1, LANES), weight[j], jnp.float32)
+
+    loop(cycles, set_weight)
+    out_row = lax.broadcasted_iota(jnp.int32, order.shape, 0)
+    in_row = lax.broadcasted_iota(jnp.int32, order.shape, 1)
+    out_slot = out_row // rows * fields + out_row % fields
+    wanted = jnp.zeros(order.shape, jnp.int32)
+    for k in range(n_cons * fields):
+        wanted = jnp.where(out_slot == k, assignment[k], wanted)
+    in_field = in_row // rows * fields + in_row % fields
+    same = (wanted == in_field) & (out_row // fields % 2 == in_row // fields % 2)
+    order[...] = jnp.where(same, 1.0, 0.0).astype(order.dtype)
+
+    def analyse(h):
+        def orders_of(shape):
+            at_lane = lax.broadcasted_iota(jnp.int32, shape, 1)
+            return at_lane // chunk_orders * (groups * GROUP) + h * chunk_orders + at_lane % chunk_orders
+
+        for ref, stride in ((coarse, near.shape[1]), (near, 1)):
+            shape = ref.shape[1:]
+            lon = lax.broadcasted_iota(jnp.int32, shape, 0) * stride
+            ref[0], ref[1] = circle((lon * orders_of(shape)).astype(jnp.float32))
+
+        def make_rows(a, carry):
+            cos_a, sin_a = coarse[0, pl.ds(a, 1), :], coarse[1, pl.ds(a, 1), :]
+            here = pl.ds(pl.multiple_of(a * near.shape[1], near.shape[1]), near.shape[1])
+            forward[here, :half_lanes] = (cos_a * near[0] - sin_a * near[1]).astype(forward.dtype)
+            forward[here, half_lanes:] = (-sin_a * near[0] - cos_a * near[1]).astype(forward.dtype)
+            return carry
+
+        lax.fori_loop(0, lens, make_rows, 0, unroll=2)
+        if h == 0:
+            for i in range(4 * per_quarter):
+                field_copy(i).wait()
+        parts = []
+        for q in range(4):
+            total = 0.0
+            for i in range(per_quarter):
+                total = total + jnp.dot(
+                    whole[q * per_quarter + i, : elevation.shape[0], :],
+                    forward[i * slot_lanes : (i + 1) * slot_lanes, :],
+                    preferred_element_type=jnp.float32,
+                )
+            parts.append((total[:, :half_lanes], total[:, half_lanes:]))
+        (re0, im0), (re1, im1), (re2, im2), (re3, im3) = parts
+        residue = lax.broadcasted_iota(jnp.int32, re0.shape, 1) % 4
+        turn_re = jnp.where(residue == 0, 1.0, jnp.where(residue == 2, -1.0, 0.0))
+        turn_im = jnp.where(residue == 1, 1.0, jnp.where(residue == 3, -1.0, 0.0))
+        sign = turn_re * turn_re - turn_im * turn_im
+        even_re, even_im = re0 + sign * re2, im0 + sign * im2
+        odd_re, odd_im = re1 + sign * re3, im1 + sign * im3
+        sums = (even_re + turn_re * odd_re + turn_im * odd_im, even_im + turn_re * odd_im - turn_im * odd_re)
+        per_tile = LANES // chunk_orders
+        for u in range(half_lanes // LANES):
+            for piece in range(2):
+                for f in range(fields):
+                    value = sums[piece][f * cycles : (f + 1) * cycles, u * LANES : (u + 1) * LANES]
+                    split_s[u, pl.ds(piece * fields + f, cycles, stride=rows), :] = value * weights[...]
+            split = split_s[u].reshape(folds, blocks, rows, LANES)
+            swapped = swap_blocks([split[:, k] for k in range(blocks)])
+            for k in range(blocks):
+                owner = u * per_tile + k // chunk
+                sent[owner * groups + h * chunk + k % chunk] = swapped[k].astype(sent.dtype)
+
+    heard = n_cons + jnp.where(p > 0, 1, 0) + jnp.where(p < chips - 1, 1, 0)
     for h in range(CHUNKS):
+        analyse(h)
+        if h == 0:
+            pl.semaphore_wait(barrier, heard)
         for k in range(n_cons - 1):
             there_copy(k, h, c).start()
 
@@ -413,7 +495,6 @@
         q = jnp.where(exports > 0, t - exports, q)
         return jnp.where(t < 2 * exports, t // 2 + back_gap, q + relay_gap) + SLACK
 
-    quarter = waves.shape[2]
     fine_rows = fine.shape[1]
     wave_blocks = waves.shape[1] // fine_rows
 
@@ -423,11 +504,7 @@
 
     def turn(row):
         lon = lax.broadcasted_iota(jnp.int32, row.shape, 1).astype(jnp.float32)
-        phase = row.astype(jnp.float32) * lon
-        period = 4.0 * quarter
-        phase = phase - jnp.floor(phase * (1.0 / period)) * period
-        angle = phase * (2.0 * 3.141592653589793 / period)
-        return jnp.cos(angle), jnp.sin(angle)
+        return circle(row.astype(jnp.float32) * lon)
 
     def make_fine():
         fine[0], fine[1] = turn(lax.broadcasted_iota(jnp.int32, (fine_rows, quarter), 0))
@@ -512,7 +589,7 @@
         merged = jnp.stack(swapped, axis=1).reshape(cycles * rows, LANES)
         out[pl.ds(pl.multiple_of(tile * cycles * rows, 8), cycles * rows), :] = merged
 
-    loop(x.shape[0], unpack)
+    loop(order_tiles, unpack)
 
     def drain_tile(t):
         pair_copy(t, corner).wait_send()
@@ -552,29 +629,33 @@
         loop(groups, lambda g, k=k: home_copy(k, g, c).wait_send())
 
 
-def exchange(x, love, order, legendre, quarter, n_cons, n_blk):
+def exchange(elevation, weight, assignment, love, legendre, n_cons, n_blk):
     cycles, orders_dev, degrees = legendre.shape
-    rows = x.shape[2]
-    all_rows = n_cons * rows
+    fields, _, longitudes = elevation.shape
+    quarter, rows = longitudes // 4, 2 * fields
+    all_rows, orders = n_cons * rows, n_cons * orders_dev
     plan = Plan(n_cons, n_blk, orders_dev, degrees)
     groups, folds = plan.groups, cycles * GROUP // LANES
     half = (GROUP * all_rows // 2, LANES)
-    kind = x.dtype
+    kind = elevation.dtype
     tiles, queue, moved = plan.max_tiles, plan.max_queue, plan.max_moved
     halves = (queue + 1) // 2
     sems = [(n,) for n in [tiles] * 2 + [moved] * 2 + [queue] * 2 + [halves] * 2 + [halves, queue, queue] + [moved] * 2 + [tiles] * 2]
     sems += [(n_cons - 1, CHUNKS), (n_cons, CHUNKS), (n_cons - 1, groups), (n_cons * groups,)]
     lane_tiles = (folds, rows, LANES)
-    waves = (2, x.shape[0] * LANES, quarter)
+    waves = (2, orders, quarter)
+    chunk_lanes = orders // CHUNKS
     vmem = pl.BlockSpec(memory_space=pltpu.VMEM)
+    scalars = pl.BlockSpec(memory_space=pltpu.SMEM)
+    anywhere = pl.BlockSpec(memory_space=pl.ANY)
     return pl.pallas_call(
         functools.partial(sum_kernel, plan),
         out_shape=[
-            jax.ShapeDtypeStruct((x.shape[0] * x.shape[1] * rows, LANES), jnp.float32),
+            jax.ShapeDtypeStruct((orders // LANES * cycles * rows, LANES), jnp.float32),
             jax.ShapeDtypeStruct(waves, kind),
         ],
-        in_specs=[vmem] * 3 + [pl.BlockSpec(memory_space=pl.ANY)],
-        out_specs=[vmem, pl.BlockSpec(memory_space=pl.ANY)],
+        in_specs=[anywhere, scalars, scalars, vmem, anywhere],
+        out_specs=[vmem, anywhere],
         scratch_shapes=[
             pltpu.VMEM((groups, cycles, GROUP, degrees), kind),
             pltpu.SemaphoreType.DMA((groups,)),
@@ -594,12 +675,25 @@
             pltpu.VMEM((2, FINE, quarter), jnp.float32),
             pltpu.VMEM(waves, kind),
             pltpu.SemaphoreType.DMA((waves[1] // FINE,)),
+            pltpu.SemaphoreType.DMA((longitudes // degrees,)),
+            pltpu.VMEM((2, quarter // FINE, chunk_lanes), jnp.float32),
+            pltpu.VMEM((2, FINE, chunk_lanes), jnp.float32),
+            pltpu.VMEM((quarter, 2 * chunk_lanes), kind),
+            pltpu.VMEM((cycles, LANES), jnp.float32),
+            pltpu.VMEM((all_rows, all_rows), kind),
+            pltpu.VMEM((chunk_lanes // LANES, cycles * rows, LANES), jnp.float32),
         ]
         + [pltpu.SemaphoreType.DMA(n) for n in sems],
         compiler_params=pltpu.CompilerParams(
             collective_id=0, has_side_effects=True, vmem_limit_bytes=60 * 2**20
         ),
-    )(x, love.reshape(degrees // LANES, LANES), order, legendre)
+    )(
+        elevation.reshape(fields * cycles, longitudes),
+        weight,
+        assignment,
+        love.reshape(degrees // LANES, LANES),
+        legendre,
+    )
 
 
 def inverse_kernel(y, wave, loading, lhs, held, result, wave_sem, out_sem):
@@ -678,68 +772,14 @@
             pltpu.SemaphoreType.DMA((parts,)),
             pltpu.SemaphoreType.DMA((parts, 4)),
         ],
-        compiler_params=pltpu.CompilerParams(vmem_limit_bytes=40 * 2**20),
+        compiler_params=pltpu.CompilerParams(vmem_limit_bytes=60 * 2**20),
     )(y, wave)
 
 
-def angles_of(lon_index, period, orders):
-    order_index = jnp.arange(orders, dtype=jnp.int32)
-    phases = lon_index[:, None] * order_index[None, :] % period
-    angles = phases.astype(jnp.float32) * jnp.float32(2.0 * 3.141592653589793 / period)
-    return jnp.cos(angles), jnp.sin(angles)
-
-
-def quarter_table(length, period, orders):
-    fine = 32
-    coarse = length // fine
-    parts = angles_of(jnp.arange(coarse, dtype=jnp.int32) * fine, period, orders)
-    parts += angles_of(jnp.arange(fine, dtype=jnp.int32), period, orders)
-    cos_a, sin_a, cos_b, sin_b = lax.optimization_barrier(parts)
-    cos_a, sin_a = cos_a[:, None, :], sin_a[:, None, :]
-    cosine = cos_a * cos_b[None] - sin_a * sin_b[None]
-    minus_sine = -(sin_a * cos_b[None] + cos_a * sin_b[None])
-    both = jnp.concatenate([cosine.astype(jnp.bfloat16), minus_sine.astype(jnp.bfloat16)], axis=2)
-    return both.reshape(length, 2 * orders)
-
-
 def local(elevation, legendre, cycle_weight, love_factor, assignment):
-    fld_dev, cycle_dev, longitudes = elevation.shape
-    orders_dev, degrees = legendre.shape[1:]
-    orders = orders_dev * lax.axis_size("cons")
-    quarter = longitudes // 4
-    table = lax.optimization_barrier(quarter_table(quarter, longitudes, orders))
-    residue = jnp.arange(orders, dtype=jnp.int32) % 4
-    turn_re = (residue == 0).astype(jnp.float32) - (residue == 2).astype(jnp.float32)
-    turn_im = (residue == 1).astype(jnp.float32) - (residue == 3).astype(jnp.float32)
-    sign = turn_re * turn_re - turn_im * turn_im
-
-    def halves(q):
-        part = lax.slice_in_dim(elevation, q * quarter, (q + 1) * quarter, axis=2)
-        both = jnp.einsum("fjk,kn->fjn", part, table, preferred_element_type=jnp.float32)
-        return both[..., :orders], both[..., orders:]
-
-    (re0, im0), (re1, im1), (re2, im2), (re3, im3) = (halves(q) for q in range(4))
-    even_re, even_im = re0 + sign * re2, im0 + sign * im2
-    odd_re, odd_im = re1 + sign * re3, im1 + sign * im3
-    running = jnp.stack(
-        [
-            even_re + turn_re * odd_re + turn_im * odd_im,
-            even_im + turn_re * odd_im - turn_im * odd_re,
-        ],
-        axis=1,
-    )
-    spectra = (running * cycle_weight[None, None, :, None]).astype(jnp.bfloat16)
-    x = spectra.reshape(fld_dev, 2, cycle_dev, orders // LANES, LANES)
-    x = x.transpose(3, 2, 1, 0, 4).reshape(orders // LANES, cycle_dev, 2 * fld_dev, LANES)
-    n_cons = lax.axis_size("cons")
-    slots = (n_cons, 2, fld_dev)
-    field = jnp.arange(n_cons * fld_dev, dtype=jnp.int32).reshape(n_cons, 1, fld_dev)
-    chosen = assignment.reshape(n_cons, 1, fld_dev)
-    piece = jnp.arange(2, dtype=jnp.int32).reshape(1, 2, 1)
-    give, have = jnp.broadcast_to(2 * field + piece, slots), jnp.broadcast_to(2 * chosen + piece, slots)
-    order = (have.reshape(-1, 1) == give.reshape(1, -1)).astype(jnp.bfloat16)
-    y, wave = exchange(x, love_factor, order, legendre, quarter, n_cons, lax.axis_size("blk"))
-    return inverse(y, wave, fld_dev, cycle_dev)
+    n_cons, n_blk = lax.axis_size("cons"), lax.axis_size("blk")
+    y, wave = exchange(elevation, cycle_weight, assignment, love_factor, legendre, n_cons, n_blk)
+    return inverse(y, wave, *elevation.shape[:2])
 
 
 def solution(mesh):

time: 129 us -> 116 us (0.90)
  local copies, waits for them, and re-layouts: 6.48 us -> 0 us
  other arithmetic: 5.39 us -> 0 us
  matrix products: 3.68 us -> 0 us
  Pallas kernels: 113 us -> 116 us
    unnamed x8 -> x0, local copies, waits for them, and re-layouts: 4.91 us -> none
    dot_general x4 -> x0, matrix products: 3.68 us -> none  [halves(): jnp.einsum('fjk,kn->fjn', part, table, preferred_element_type=jnp.float32)]
    convert_element_type x2 -> x0, other arithmetic: 2.78 us -> none  [the longest x1 2.11 us: quarter_table(): cosine.astype(jnp.bfloat16)]
    pallas_call x1, Pallas kernels: 107 us -> 109 us  [exchange(): pl.pallas_call(functools.partial(sum_kernel, plan), out_shape=[jax.ShapeD...]
    pallas_call x1, Pallas kernels: 5.91 us -> 7.48 us  [inverse(): pl.pallas_call(inverse_kernel, out_shape=jax.ShapeDtypeStruct((fields, cy...]
where the time goes in v2:
time: 116 us
  Pallas kernels  116 us (100%)
    pallas_call x1, Pallas kernels, exchange(): pl.pallas_call(functools.partial(sum_kernel, plan), out_shape=[jax.ShapeD...  109 us
    pallas_call x1, Pallas kernels, inverse(): pl.pallas_call(inverse_kernel, out_shape=jax.ShapeDtypeStruct((fields, cy...  7.48 us

profile of v2, /device:TPU:1, one launch (start us, length us, event | category | flops | bytes accessed | tf_op | source)
XLA Modules:
  0.0 116.1 jit_solution(11536716968378013059)
XLA Ops:
  0.0 108.6 %shard_map.55 = (f32[1920,128]{1,0:T(8,128)}, bf16[2,768,1536]{2,1,0:T(8,128)(2,1)}) custom-call(bf16[160,6144]{1,0:T(8,128)(2,1)} %bitcast.2, f32[40]{0:T(128)} %weight.1, s32[16]{0:T(128)} %assignment.1, f32[6,128]{1,0:T(8,128)} %bitcast.3, bf16[40,192,768]{2,1,0:T(8,128)(2,1)} %legendre.1), custom_call_target="tpu_custom_call" | custom-call | tf_op jit(solution)/shard_map/pallas_call | solution.py:651
  108.7 7.5 %shard_map.56 = f32[4,40,6144]{2,1,0:T(8,128)} custom-call(f32[1920,128]{1,0:T(8,128)} %get-tuple-element.7.y, bf16[2,768,1536]{2,1,0:T(8,128)(2,1)} %get-tuple-element.8.wave), custom_call_target="tpu_custom_call" | custom-call | tf_op jit(solution)/shard_map/pallas_call | solution.py:763

commit v3 on v2

--- a/solution.py
+++ b/solution.py
@@ -9,17 +9,20 @@
 
 GROUP = 16
 LANES = 128
-LEAD = 6
+LEAD = 4
 FIN = 4
 REL0 = 8
 REL1 = 14
 RELN = 5
 BACK = 4
 SLACK = 2
-AHEAD = 2
-PACE = 3
+AHEAD = 1
+PACE = 2
+EARLY = 2
+CHUNK_AT = 3
 CHUNKS = 3
-WAVE_AT = 1
+VMEM_MIB = 60
+WAVE_AT = 5
 FINE = 32
 MESH = pl.DeviceIdType.MESH
 
@@ -40,24 +43,41 @@
     def first(self, c, g):
         return (c * self.groups + g) * GROUP // LANES
 
+    def turn(self, c, g):
+        return (c * self.groups + g) % (LANES // GROUP)
+
+    def mate(self, c, g):
+        return g + LANES // GROUP - 2 * self.turn(c, g)
+
+    def merged(self, c, g):
+        return (self.turn(c, g) > LANES // GROUP // 2) & (self.mate(c, g) >= 0)
+
+    def lost(self, c, g):
+        place = self.turn(c, g)
+        return (place > 0) & (place < LANES // GROUP // 2) & (self.mate(c, g) < self.groups)
+
     def width(self, c, g):
-        return self.columns - self.first(c, g)
+        return self.columns - self.first(c, g) - (1 if self.lost(c, g) else 0)
 
     def starts(self, c):
-        begin, out = 0, []
-        for g in range(self.groups):
-            out.append(begin)
-            begin = begin + self.width(c, g)
-        return out, begin
+        sums = []
+        for k in range(self.groups + 1):
+            sums.append(pick(c, [sum(self.width(b, g) for g in range(k)) for b in range(self.n_cons)]))
+        return sums[:-1], sums[-1]
 
     def place(self, c, starts, t):
-        g = 0
-        for start in starts[1:]:
-            g = g + jnp.where(t >= start, 1, 0)
-        begin = 0
+        starts, tiles = starts
+        g, end = 0, starts[1]
         for k in range(1, self.groups):
-            begin = jnp.where(t >= starts[k], starts[k], begin)
-        return g, (c * self.groups + g) * GROUP // LANES + t - begin
+            after = starts[k + 1] if k + 1 < self.groups else tiles
+            g = g + jnp.where(t >= starts[k], 1, 0)
+            end = jnp.where(t >= starts[k], after, end)
+        return g, self.columns - end + t
+
+    def shift(self, c, spot):
+        g, lt = spot
+        joined = self.merged(c, g) & (lt == self.first(c, g))
+        return jnp.where(joined, LANES - GROUP * self.turn(c, g), 0)
 
 
 def pick(c, values):
@@ -115,8 +135,8 @@
     other_c = n_cons - 1 - c
     last = mid - 1
 
-    starts, tiles = plan.starts(c)
-    other_starts, _ = plan.starts(other_c)
+    listed, other_starts = plan.starts(c), plan.starts(other_c)
+    starts, tiles = listed
     exports, imports = pick(c, plan.moved), pick(other_c, plan.moved)
     queue = pick(c, plan.queues)
 
@@ -172,6 +192,7 @@
     period = 4.0 * quarter
     slot_lanes = whole.shape[2]
     per_quarter = quarter // slot_lanes
+    base = groups - 4 * per_quarter
     chunk_orders = chunk * GROUP
     half_lanes = n_cons * chunk_orders
     lens = coarse.shape[1]
@@ -184,7 +205,7 @@
     def field_copy(i):
         lanes = pl.ds(i * slot_lanes, slot_lanes)
         return pltpu.make_async_copy(
-            elevation.at[:, lanes], whole.at[i, pl.ds(0, elevation.shape[0]), :], field_sem.at[i]
+            elevation.at[:, lanes], part.at[base + i, pl.ds(0, elevation.shape[0]), :], field_sem.at[i]
         )
 
     for i in range(4 * per_quarter):
@@ -222,7 +243,7 @@
             forward[here, half_lanes:] = (-sin_a * near[0] - cos_a * near[1]).astype(forward.dtype)
             return carry
 
-        lax.fori_loop(0, lens, make_rows, 0, unroll=2)
+        lax.fori_loop(0, lens, make_rows, 0, unroll=8)
         if h == 0:
             for i in range(4 * per_quarter):
                 field_copy(i).wait()
@@ -231,7 +252,7 @@
             total = 0.0
             for i in range(per_quarter):
                 total = total + jnp.dot(
-                    whole[q * per_quarter + i, : elevation.shape[0], :],
+                    part[base + q * per_quarter + i, : elevation.shape[0], :],
                     forward[i * slot_lanes : (i + 1) * slot_lanes, :],
                     preferred_element_type=jnp.float32,
                 )
@@ -257,17 +278,18 @@
                 sent[owner * groups + h * chunk + k % chunk] = swapped[k].astype(sent.dtype)
 
     heard = n_cons + jnp.where(p > 0, 1, 0) + jnp.where(p < chips - 1, 1, 0)
-    for h in range(CHUNKS):
+
+    def send_chunk(h):
         analyse(h)
         if h == 0:
             pl.semaphore_wait(barrier, heard)
         for k in range(n_cons - 1):
             there_copy(k, h, c).start()
-
-    def keep(g):
-        taken[c, g] = sent[c * groups + g]
-
-    loop(groups, keep)
+        for g in range(h * chunk, (h + 1) * chunk):
+            taken[c, g] = sent[c * groups + g]
+
+    for h in range(min(EARLY, CHUNKS)):
+        send_chunk(h)
 
     def home_copy(k, g, source):
         return copy(
@@ -381,7 +403,17 @@
             ).astype(part.dtype)
 
         span(first_of(g) // 2, pairs, one)
-        span(start_of(g), start_of(g + 1), lambda t: pair_copy(t, plan.place(c, starts, t)).start())
+
+        @pl.when(plan.merged(c, g))
+        def _():
+            here = pl.ds(pl.multiple_of(first_of(g) * LANES, LANES), LANES)
+            moved = LANES - GROUP * plan.turn(c, g)
+            lanes = lax.broadcasted_iota(jnp.int32, (2 * half, LANES), 1)
+            low = pltpu.roll(part[g, :, here].astype(jnp.float32), moved, 1)
+            high = part[plan.mate(c, g), :, here].astype(jnp.float32)
+            part[g, :, here] = jnp.where(lanes < moved, low, high).astype(part.dtype)
+
+        span(start_of(g), start_of(g + 1), lambda t: pair_copy(t, plan.place(c, listed, t)).start())
 
     width = folds * LANES
     order_lane = lax.broadcasted_iota(jnp.int32, (rows, LANES), 1) % GROUP
@@ -391,7 +423,21 @@
             fin_copy(t, corner).wait_recv()
 
         span(start_of(g), start_of(g + 1), take)
-
+        joined = plan.merged(c, g)
+
+        @pl.when(joined)
+        def _():
+            here = pl.ds(pl.multiple_of(first_of(g) * LANES, LANES), LANES)
+            fin_copy(start_of(g), corner).wait_send()
+            both = whole[g, :, here]
+            whole[plan.mate(c, g), :, here] = both
+            back_by = GROUP * plan.turn(c, g)
+            whole[g, :, here] = pltpu.roll(both.astype(jnp.float32), back_by, 1).astype(whole.dtype)
+
+        count = jnp.where(plan.lost(c, g), 0, jnp.where(joined, 2, 1))
+        span(0, count, lambda n: synthesise(jnp.where(n == 0, g, plan.mate(c, g))))
+
+    def synthesise(g):
         def one(lp, total):
             values = table[g, :, :, lane_pair(lp)].reshape(cycles * GROUP, 2 * LANES)
             full = lax.dot_general(
@@ -414,7 +460,7 @@
         returned[c * groups + g] = back[g, c]
 
     def give(e):
-        spot = plan.place(c, starts, 2 * e)
+        spot = plan.place(c, listed, 2 * e)
         pair_copy(2 * e, spot).wait_recv()
         given[e] = add(at(part, spot, mine)[...], pair_in[2 * e]).astype(given.dtype)
         give_copy(e).start()
@@ -425,7 +471,7 @@
         @pl.when(native)
         def _():
             t = tile_of(q)
-            spot = plan.place(c, starts, t)
+            spot = plan.place(c, listed, t)
             pair_copy(t, spot).wait_recv()
             acc[q] = add(at(part, spot, mine)[...], pair_in[t]).astype(acc.dtype)
 
@@ -459,7 +505,7 @@
         @pl.when(jnp.logical_not(is_import(q)))
         def _():
             t = tile_of(q)
-            spot = plan.place(c, starts, t)
+            spot = plan.place(c, listed, t)
             at(whole, spot, mine)[...] = coef[q]
             fin_copy(t, spot).start()
 
@@ -467,10 +513,14 @@
         @pl.when((depth == 0) & (lax.rem(q, 2) == side))
         def _():
             cross_copy(q).wait_recv()
-            own = plan.place(c, starts, tile_of(q))[1]
-            lent = plan.place(other_c, other_starts, 2 * (q - LEAD))[1]
-            lt = jnp.where(is_import(q), lent, own)
-            total = add(acc[q], cross_in[q // 2]) * love[pl.ds(lt, 1), :]
+            own = plan.place(c, listed, tile_of(q))
+            lent = plan.place(other_c, other_starts, 2 * (q - LEAD))
+            lt = jnp.where(is_import(q), lent[1], own[1])
+            moved = jnp.where(is_import(q), plan.shift(other_c, lent), plan.shift(c, own))
+            scale = jnp.broadcast_to(love[pl.ds(lt, 1), :], (8, LANES))
+            ahead_of = lax.broadcasted_iota(jnp.int32, (8, LANES), 1) < moved
+            scale = jnp.where(ahead_of, pltpu.roll(scale, moved, 1), scale)[:1]
+            total = add(acc[q], cross_in[q // 2]) * scale
             coef[q] = total.astype(coef.dtype)
             mid_copy(q).start()
             spread(q)
@@ -482,7 +532,7 @@
             spread(q)
 
     def take_back(e):
-        spot = plan.place(c, starts, 2 * e)
+        spot = plan.place(c, listed, 2 * e)
         ret_copy(0, e, spot).wait_recv()
         fin_copy(2 * e, spot).start()
 
@@ -491,9 +541,9 @@
 
     def ready(g):
         t = start_of(g + 1) - 1
-        q = jnp.where(t >= LEAD, t + imports, t)
-        q = jnp.where(exports > 0, t - exports, q)
-        return jnp.where(t < 2 * exports, t // 2 + back_gap, q + relay_gap) + SLACK
+        q = jnp.where(t < 2 * exports, t // 2, t - exports) + jnp.where(t >= LEAD, imports, 0)
+        e = jnp.where(start_of(g) < 2 * exports, jnp.minimum(t // 2, exports - 1) + back_gap, 0)
+        return jnp.maximum(q + relay_gap, e) + SLACK
 
     fine_rows = fine.shape[1]
     wave_blocks = waves.shape[1] // fine_rows
@@ -521,6 +571,12 @@
         produce(g)
 
     def step(i, done):
+        for h in range(EARLY, CHUNKS):
+
+            @pl.when(i == CHUNK_AT + (h - EARLY) * 4)
+            def _(h=h):
+                send_chunk(h)
+
         @pl.when(i == WAVE_AT)
         def _():
             make_fine()
@@ -593,9 +649,14 @@
 
     def drain_tile(t):
         pair_copy(t, corner).wait_send()
-        fin_copy(t, corner).wait_send()
 
     loop(tiles, drain_tile)
+
+    def drain_group(g):
+        begin = start_of(g) + jnp.where(plan.merged(c, g), 1, 0)
+        span(begin, start_of(g + 1), lambda t: fin_copy(t, corner).wait_send())
+
+    loop(groups, drain_group)
     loop(exports, lambda e: give_copy(e).wait_send())
 
     def drain_queue(q):
@@ -685,7 +746,7 @@
         ]
         + [pltpu.SemaphoreType.DMA(n) for n in sems],
         compiler_params=pltpu.CompilerParams(
-            collective_id=0, has_side_effects=True, vmem_limit_bytes=60 * 2**20
+            collective_id=0, has_side_effects=True, vmem_limit_bytes=VMEM_MIB * 2**20
         ),
     )(
         elevation.reshape(fields * cycles, longitudes),

time: 116 us -> 114 us (0.983)
  Pallas kernels: 116 us -> 114 us
    pallas_call x1, Pallas kernels: 109 us -> 106 us  [exchange(): pl.pallas_call(functools.partial(sum_kernel, plan), out_shape=[jax.ShapeD...]
where the time goes in v3:
time: 114 us
  Pallas kernels  114 us (100%)
    pallas_call x1, Pallas kernels, exchange(): pl.pallas_call(functools.partial(sum_kernel, plan), out_shape=[jax.ShapeD...  106 us
    pallas_call x1, Pallas kernels, inverse(): pl.pallas_call(inverse_kernel, out_shape=jax.ShapeDtypeStruct((fields, cy...  7.48 us

profile of v3, /device:TPU:1, one launch (start us, length us, event | category | flops | bytes accessed | tf_op | source)
XLA Modules:
  0.0 113.8 jit_solution(247661192129856337)
XLA Ops:
  0.0 106.3 %shard_map.55 = (f32[1920,128]{1,0:T(8,128)}, bf16[2,768,1536]{2,1,0:T(8,128)(2,1)}) custom-call(bf16[160,6144]{1,0:T(8,128)(2,1)} %bitcast.2, f32[40]{0:T(128)} %weight.1, s32[16]{0:T(128)} %assignment.1, f32[6,128]{1,0:T(8,128)} %bitcast.3, bf16[40,192,768]{2,1,0:T(8,128)(2,1)} %legendre.1), custom_call_target="tpu_custom_call" | custom-call | tf_op jit(solution)/shard_map/pallas_call | solution.py:712
  106.3 7.5 %shard_map.56 = f32[4,40,6144]{2,1,0:T(8,128)} custom-call(f32[1920,128]{1,0:T(8,128)} %get-tuple-element.7.y, bf16[2,768,1536]{2,1,0:T(8,128)(2,1)} %get-tuple-element.8.wave), custom_call_target="tpu_custom_call" | custom-call | tf_op jit(solution)/shard_map/pallas_call | solution.py:824

commit v4 on v3

--- a/solution.py
+++ b/solution.py
@@ -18,9 +18,11 @@
 SLACK = 2
 AHEAD = 1
 PACE = 2
-EARLY = 2
+EARLY = 3
 CHUNK_AT = 3
+CHUNK_EVERY = 1
 CHUNKS = 3
+WIDE = 6
 VMEM_MIB = 60
 WAVE_AT = 5
 FINE = 32
@@ -107,9 +109,9 @@
 
 
 def sum_kernel(
-    plan, elevation, weight, assignment, love, legendre, out, wave, table, table_sem, part, spread_s, whole, sent, taken, back, returned,
+    plan, elevation, weight, assignment, love, legendre, y, wave, table, table_sem, part, spread_s, whole, sent, taken, back, returned,
     pair_in, acc, given, inward_in, cross_in, coef, fine, waves, wave_sem,
-    field_sem, coarse, near, forward, weights, order, split_s, *sems
+    out, out_sem, field_sem, coarse, near, forward, weights, order, split_s, *sems
 ):
     (pair_s, pair_r, give_s, give_r, in_s, in_r, cross_s, cross_r, mid_s, out_s, coef_r, ret_s, ret_r, fin_s, fin_r) = sems[:15]
     there_s, there_r, home_s, home_r = sems[15:]
@@ -192,7 +194,7 @@
     period = 4.0 * quarter
     slot_lanes = whole.shape[2]
     per_quarter = quarter // slot_lanes
-    base = groups - 4 * per_quarter
+    base, field_rows = groups - 2 * per_quarter, elevation.shape[0]
     chunk_orders = chunk * GROUP
     half_lanes = n_cons * chunk_orders
     lens = coarse.shape[1]
@@ -204,8 +206,10 @@
 
     def field_copy(i):
         lanes = pl.ds(i * slot_lanes, slot_lanes)
+        q, piece = i // per_quarter, i % per_quarter
+        here = pl.ds(q % 2 * field_rows, field_rows)
         return pltpu.make_async_copy(
-            elevation.at[:, lanes], part.at[base + i, pl.ds(0, elevation.shape[0]), :], field_sem.at[i]
+            elevation.at[:, lanes], part.at[base + q // 2 * per_quarter + piece, here, :], field_sem.at[i]
         )
 
     for i in range(4 * per_quarter):
@@ -248,15 +252,16 @@
             for i in range(4 * per_quarter):
                 field_copy(i).wait()
         parts = []
-        for q in range(4):
+        for q in range(2):
             total = 0.0
             for i in range(per_quarter):
                 total = total + jnp.dot(
-                    part[base + q * per_quarter + i, : elevation.shape[0], :],
+                    part[base + q * per_quarter + i, : 2 * field_rows, :],
                     forward[i * slot_lanes : (i + 1) * slot_lanes, :],
                     preferred_element_type=jnp.float32,
                 )
-            parts.append((total[:, :half_lanes], total[:, half_lanes:]))
+            for piece in (total[:field_rows], total[field_rows:]):
+                parts.append((piece[:, :half_lanes], piece[:, half_lanes:]))
         (re0, im0), (re1, im1), (re2, im2), (re3, im3) = parts
         residue = lax.broadcasted_iota(jnp.int32, re0.shape, 1) % 4
         turn_re = jnp.where(residue == 0, 1.0, jnp.where(residue == 2, -1.0, 0.0))
@@ -365,7 +370,7 @@
 
         lax.fori_loop(begin, end, step, 0)
 
-    lane = lax.broadcasted_iota(jnp.int32, (all_rows, LANES), 1) % GROUP
+    lane = lax.broadcasted_iota(jnp.int32, (all_rows, folds * LANES), 1) % GROUP
 
     def clear(g):
         first = first_of(g)
@@ -387,14 +392,13 @@
                     there_copy(0, g // chunk, source).wait_recv()
 
         table_copy(g).wait()
-        for fold in range(folds):
-            parts = [taken[source, g, fold].astype(jnp.float32) for source in range(n_cons)]
-            gathered = jnp.concatenate(parts, axis=0).astype(jnp.bfloat16)
-            ordered = jnp.dot(order[...], gathered, preferred_element_type=jnp.float32)
-            for m in range(GROUP):
-                spread_s[pl.ds(m * all_rows, all_rows), pl.ds(fold * LANES, LANES)] = jnp.where(
-                    lane == m, ordered, 0.0
-                ).astype(spread_s.dtype)
+        lists = [
+            jnp.concatenate([taken[source, g, fold] for source in range(n_cons)], axis=0) for fold in range(folds)
+        ]
+        gathered = jnp.concatenate(lists, axis=1)
+        ordered = jnp.dot(order[...], gathered, preferred_element_type=jnp.float32)
+        for m in range(GROUP):
+            spread_s[pl.ds(m * all_rows, all_rows), :] = jnp.where(lane == m, ordered, 0.0).astype(spread_s.dtype)
 
         def one(lp):
             values = table[g, :, :, lane_pair(lp)].reshape(cycles * GROUP, 2 * LANES)
@@ -571,9 +575,35 @@
         produce(g)
 
     def step(i, done):
+        @pl.when(i < exports)
+        def _():
+            give(i)
+
+        @pl.when(i < queue)
+        def _():
+            gather(i)
+
+        q = i - FIN
+
+        @pl.when((q >= 0) & (q < queue))
+        def _():
+            finish(q)
+
+        r = i - relay_gap
+
+        @pl.when((r >= 0) & (r < queue))
+        def _():
+            relay(r)
+
+        e = i - back_gap
+
+        @pl.when((e >= 0) & (e < exports))
+        def _():
+            take_back(e)
+
         for h in range(EARLY, CHUNKS):
 
-            @pl.when(i == CHUNK_AT + (h - EARLY) * 4)
+            @pl.when(i == CHUNK_AT + (h - EARLY) * CHUNK_EVERY)
             def _(h=h):
                 send_chunk(h)
 
@@ -593,33 +623,7 @@
         def _():
             produce(ahead)
 
-        @pl.when(i < exports)
-        def _():
-            give(i)
-
-        @pl.when(i < queue)
-        def _():
-            gather(i)
-
-        q = i - FIN
-
-        @pl.when((q >= 0) & (q < queue))
-        def _():
-            finish(q)
-
-        r = i - relay_gap
-
-        @pl.when((r >= 0) & (r < queue))
-        def _():
-            relay(r)
-
-        e = i - back_gap
-
-        @pl.when((e >= 0) & (e < exports))
-        def _():
-            take_back(e)
-
-        now = (done < groups) & (i >= ready(done))
+        now = (done < groups) & (i >= ready(done)) & ((lax.rem(i, PACE) > 0) | (i > PACE * groups))
 
         @pl.when(now)
         def _():
@@ -630,22 +634,6 @@
     count = plan.max_queue + LEAD + REL1 + mid * RELN + BACK
     done = lax.fori_loop(0, count, step, 0)
     span(done, groups, restore)
-
-    def unpack(tile):
-        def heard_from(k):
-            index = tile * blocks + k
-
-            @pl.when(index // groups != c)
-            def _():
-                home_copy(0, lax.rem(index, groups), index // groups).wait_recv()
-
-        loop(blocks, heard_from)
-
-        swapped = swap_blocks([returned[tile * blocks + k].astype(jnp.float32) for k in range(blocks)])
-        merged = jnp.stack(swapped, axis=1).reshape(cycles * rows, LANES)
-        out[pl.ds(pl.multiple_of(tile * cycles * rows, 8), cycles * rows), :] = merged
-
-    loop(order_tiles, unpack)
 
     def drain_tile(t):
         pair_copy(t, corner).wait_send()
@@ -688,6 +676,32 @@
             there_copy(k, h, c).wait_send()
 
         loop(groups, lambda g, k=k: home_copy(k, g, c).wait_send())
+
+    def tile_rows(tile):
+        return pl.ds(pl.multiple_of(tile * cycles * rows, 8), cycles * rows)
+
+    def y_copy(tile):
+        return pltpu.make_async_copy(out.at[tile_rows(tile), :], y.at[tile_rows(tile), :], out_sem.at[tile])
+
+    def unpack(tile):
+        def heard_from(k):
+            index = tile * blocks + k
+
+            @pl.when(index // groups != c)
+            def _():
+                home_copy(0, lax.rem(index, groups), index // groups).wait_recv()
+
+        loop(blocks, heard_from)
+
+        swapped = swap_blocks([returned[tile * blocks + k].astype(jnp.float32) for k in range(blocks)])
+        merged = jnp.stack(swapped, axis=1).reshape(cycles * rows, LANES)
+        out[tile_rows(tile), :] = merged
+        y_copy(tile).start()
+
+    latest = [max(k % groups for k in range(t * blocks, (t + 1) * blocks)) for t in range(order_tiles)]
+    turns = sorted(range(order_tiles), key=lambda t: latest[t])
+    loop(order_tiles, lambda n: unpack(pick(n, turns)))
+    loop(order_tiles, lambda t: y_copy(t).wait())
 
 
 def exchange(elevation, weight, assignment, love, legendre, n_cons, n_blk):
@@ -716,7 +730,7 @@
             jax.ShapeDtypeStruct(waves, kind),
         ],
         in_specs=[anywhere, scalars, scalars, vmem, anywhere],
-        out_specs=[vmem, anywhere],
+        out_specs=[anywhere, anywhere],
         scratch_shapes=[
             pltpu.VMEM((groups, cycles, GROUP, degrees), kind),
             pltpu.SemaphoreType.DMA((groups,)),
@@ -736,6 +750,8 @@
             pltpu.VMEM((2, FINE, quarter), jnp.float32),
             pltpu.VMEM(waves, kind),
             pltpu.SemaphoreType.DMA((waves[1] // FINE,)),
+            pltpu.VMEM((orders // LANES * cycles * rows, LANES), jnp.float32),
+            pltpu.SemaphoreType.DMA((orders // LANES,)),
             pltpu.SemaphoreType.DMA((longitudes // degrees,)),
             pltpu.VMEM((2, quarter // FINE, chunk_lanes), jnp.float32),
             pltpu.VMEM((2, FINE, chunk_lanes), jnp.float32),
@@ -757,7 +773,7 @@
     )
 
 
-def inverse_kernel(y, wave, loading, lhs, held, result, wave_sem, out_sem):
+def inverse_kernel(given, wave, loading, y, lhs, held, result, y_sem, wave_sem, out_sem):
     fields, cycles, longitudes = loading.shape
     quarter, tiles = longitudes // 4, lhs.shape[1] // LANES
     width, parts = held.shape[3], held.shape[0]
@@ -775,6 +791,12 @@
             result.at[n, pl.ds(q * fields, fields)], loading.at[:, :, place], out_sem.at[n, q]
         )
 
+    def y_copy(tile):
+        here = pl.ds(tile * cycles * rows, cycles * rows)
+        return pltpu.make_async_copy(given.at[here, :], y.at[here, :], y_sem.at[tile])
+
+    for tile in range(tiles // 2):
+        y_copy(tile).start()
     for n in range(parts):
         wave_copy(n).start()
     residue = lax.broadcasted_iota(jnp.int32, (2 * cycles, LANES), 1) % 4
@@ -783,6 +805,7 @@
     sign = turn_re * turn_re - turn_im * turn_im
     orders = tiles * LANES // 2
     for tile in range(tiles // 2):
+        y_copy(tile).wait()
 
         def load(piece, pair):
             at = [tile * cycles * rows + piece * fields + 2 * pair + k for k in range(2)]
@@ -819,17 +842,20 @@
 
 def inverse(y, wave, fields, cycles):
     orders, quarter = wave.shape[1:]
-    parts = quarter // (2 * LANES)
+    width = WIDE * LANES
+    parts = quarter // width
     anywhere = pl.BlockSpec(memory_space=pl.ANY)
     return pl.pallas_call(
         inverse_kernel,
         out_shape=jax.ShapeDtypeStruct((fields, cycles, 4 * quarter), jnp.float32),
-        in_specs=[pl.BlockSpec(memory_space=pltpu.VMEM), anywhere],
+        in_specs=[anywhere, anywhere],
         out_specs=anywhere,
         scratch_shapes=[
+            pltpu.VMEM(y.shape, jnp.float32),
             pltpu.VMEM((4 * fields * cycles, 2 * orders), jnp.bfloat16),
-            pltpu.VMEM((parts, 2, orders, 2 * LANES), jnp.bfloat16),
-            pltpu.VMEM((parts, 4 * fields, cycles, 2 * LANES), jnp.float32),
+            pltpu.VMEM((parts, 2, orders, width), jnp.bfloat16),
+            pltpu.VMEM((parts, 4 * fields, cycles, width), jnp.float32),
+            pltpu.SemaphoreType.DMA((orders // LANES,)),
             pltpu.SemaphoreType.DMA((parts,)),
             pltpu.SemaphoreType.DMA((parts, 4)),
         ],

time: 114 us -> 112 us (0.982)
  Pallas kernels: 114 us -> 112 us
    pallas_call x1, Pallas kernels: 106 us -> 105 us  [exchange(): pl.pallas_call(functools.partial(sum_kernel, plan), out_shape=[jax.ShapeD...]
where the time goes in v4:
time: 112 us
  Pallas kernels  112 us (100%)
    pallas_call x1, Pallas kernels, exchange(): pl.pallas_call(functools.partial(sum_kernel, plan), out_shape=[jax.ShapeD...  105 us
    pallas_call x1, Pallas kernels, inverse(): pl.pallas_call(inverse_kernel, out_shape=jax.ShapeDtypeStruct((fields, cy...  6.85 us

profile of v4, /device:TPU:1, one launch (start us, length us, event | category | flops | bytes accessed | tf_op | source)
XLA Modules:
  0.0 111.6 jit_solution(9507456781581871325)
XLA Ops:
  0.0 104.7 %shard_map.55 = (f32[1920,128]{1,0:T(8,128)}, bf16[2,768,1536]{2,1,0:T(8,128)(2,1)}) custom-call(bf16[160,6144]{1,0:T(8,128)(2,1)} %bitcast.2, f32[40]{0:T(128)} %weight.1, s32[16]{0:T(128)} %assignment.1, f32[6,128]{1,0:T(8,128)} %bitcast.3, bf16[40,192,768]{2,1,0:T(8,128)(2,1)} %legendre.1), custom_call_target="tpu_custom_call" | custom-call | tf_op jit(solution)/shard_map/pallas_call | solution.py:726
  104.7 6.8 %shard_map.56 = f32[4,40,6144]{2,1,0:T(8,128)} custom-call(f32[1920,128]{1,0:T(8,128)} %get-tuple-element.7.given, bf16[2,768,1536]{2,1,0:T(8,128)(2,1)} %get-tuple-element.8.wave), custom_call_target="tpu_custom_call" | custom-call | tf_op jit(solution)/shard_map/pallas_call | solution.py:848

commit v5 on v4

--- a/solution.py
+++ b/solution.py
@@ -14,8 +14,8 @@
 REL0 = 8
 REL1 = 14
 RELN = 5
-BACK = 4
-SLACK = 2
+BACK = 3
+SLACK = 1
 AHEAD = 1
 PACE = 2
 EARLY = 3

time: 112 us -> 112 us (level)
  no operation moved by 1% of the time
where the time goes in v5:
time: 112 us; the launch traced here: 111 us
  Pallas kernels  111 us (99%)
    pallas_call x1, Pallas kernels, exchange(): pl.pallas_call(functools.partial(sum_kernel, plan), out_shape=[jax.ShapeD...  104 us
    pallas_call x1, Pallas kernels, inverse(): pl.pallas_call(inverse_kernel, out_shape=jax.ShapeDtypeStruct((fields, cy...  6.85 us

profile of v5, /device:TPU:1, one launch (start us, length us, event | category | flops | bytes accessed | tf_op | source)
XLA Modules:
  0.0 111.4 jit_solution(8020488417871683706)
XLA Ops:
  0.0 104.5 %shard_map.55 = (f32[1920,128]{1,0:T(8,128)}, bf16[2,768,1536]{2,1,0:T(8,128)(2,1)}) custom-call(bf16[160,6144]{1,0:T(8,128)(2,1)} %bitcast.2, f32[40]{0:T(128)} %weight.1, s32[16]{0:T(128)} %assignment.1, f32[6,128]{1,0:T(8,128)} %bitcast.3, bf16[40,192,768]{2,1,0:T(8,128)(2,1)} %legendre.1), custom_call_target="tpu_custom_call" | custom-call | tf_op jit(solution)/shard_map/pallas_call | solution.py:726
  104.5 6.8 %shard_map.56 = f32[4,40,6144]{2,1,0:T(8,128)} custom-call(f32[1920,128]{1,0:T(8,128)} %get-tuple-element.7.given, bf16[2,768,1536]{2,1,0:T(8,128)(2,1)} %get-tuple-element.8.wave), custom_call_target="tpu_custom_call" | custom-call | tf_op jit(solution)/shard_map/pallas_call | solution.py:848
